TPU v7x, 32 devices: a whole 2x2x4 slice. The times are simulated.
32 devices in a mesh: xy: 2 (over core), gz: 4 (over y, x), ta: 4 (over z).
Axes of the slice: x: 2, y: 2, z: 4, core: 2. Of those that a mesh axis runs over, the one named last changes fastest.
Arguments:
- right_side: float32 [2, 4, 4, 128, 128], P('xy', 'gz', 'ta'), may hold values from -40 to 40
- link_blocks: float32 [2, 4, 4, 9, 2, 32, 32, 128], P('xy', 'gz', 'ta'), may hold values from -0.75 to 0.75
Outputs:
- solution: float32 [2, 4, 4, 128, 128], P('xy', 'gz', 'ta')
- residual: float32 [2, 4, 4, 128, 128], P('xy', 'gz', 'ta')
All inputs are finite; a program needn't handle non-finite values.
Results may differ from a plain program's by a relative error of at most 0.00018.
Values sent between devices are 32-bit elements; how exact they have to be, the bound alone decides.
No kernel may reach another device: no remote copies, remote signals or barrier semaphores. Data moves between devices by JAX's collectives and lax.ppermute only.
A program may use at most 128 MiB of HBM per device.

v0:
```python
import jax
import jax.numpy as jnp
from jax import lax
from jax.experimental import pallas as pl
from jax.experimental.pallas import tpu as pltpu
from jax.sharding import PartitionSpec as P


DOF = 32
RHS = 2
CX = 1
NY = 8
CZ = 2
CT = 8
S = CX * NY * CZ * CT
VEC = RHS * 2 * DOF
SUB = 8
TILES = DOF // SUB
AXES = ("xy", "gz", "ta")

mass_shift = 4.0
epsilon = 1e-06
f32 = jnp.float32
FIRST_COST = 20_000_000_000

VMEM_SPEC = pl.BlockSpec(memory_space=pltpu.VMEM)
PARAMS = pltpu.CompilerParams(vmem_limit_bytes=12 * 1024 * 1024)


def call(body, outs, scratch=(), cost=None):
    if cost is not None:
        cost = pl.CostEstimate(flops=cost, bytes_accessed=0, transcendentals=0)
    return pl.pallas_call(
        body,
        out_shape=[jax.ShapeDtypeStruct(o, f32) for o in outs],
        out_specs=[VMEM_SPEC] * len(outs),
        scratch_shapes=list(scratch),
        compiler_params=PARAMS,
        cost_estimate=cost,
    )


def swap_halves(axis, first, second):
    odd = lax.axis_index(axis) % 2 == 1
    return jnp.where(odd, second, first), jnp.where(odd, first, second)


def write_faces(src_ref, za_ref, zb_ref, ta_ref, tb_ref):
    pairs = src_ref[...].reshape(NY, CZ * CT, VEC)
    low = pairs[:, :CT].reshape(NY * CT, VEC)
    high = pairs[:, (CZ - 1) * CT :].reshape(NY * CT, VEC)
    za_ref[...], zb_ref[...] = swap_halves("gz", high, low)
    rows = S // CT
    low = src_ref[pl.ds(0, rows, stride=CT), :]
    high = src_ref[pl.ds(CT - 1, rows, stride=CT), :]
    ta_ref[...], tb_ref[...] = swap_halves("ta", high, low)


FACES = ((NY * CT, VEC), (NY * CT, VEC), (S // CT, VEC), (S // CT, VEC))


def faces_body(src_ref, *outs):
    write_faces(src_ref, *outs)


def multiply(fields, links, groups, red, out, add=None):
    def chunk(cb, carry):
        acc = [None] * (2 * RHS * SUB)
        for field, dirs in groups:
            for tile in range(TILES):
                x = [
                    fields[field, part * DOF + tile * SUB : part * DOF + (tile + 1) * SUB, :]
                    for part in range(2 * RHS)
                ]
                rows = pl.ds(tile * SUB, SUB)
                for c in range(SUB):
                    lr = links[dirs[0], 0, cb * SUB + c, rows, :]
                    li = links[dirs[0], 1, cb * SUB + c, rows, :]
                    for k in dirs[1:]:
                        lr = lr + links[k, 0, cb * SUB + c, rows, :]
                        li = li + links[k, 1, cb * SUB + c, rows, :]
                    for r in range(RHS):
                        re = lr * x[2 * r] - li * x[2 * r + 1]
                        im = lr * x[2 * r + 1] + li * x[2 * r]
                        for part, value in ((2 * r, re), (2 * r + 1, im)):
                            slot = part * SUB + c
                            acc[slot] = value if acc[slot] is None else acc[slot] + value
        for slot, value in enumerate(acc):
            red[slot * SUB : (slot + 1) * SUB, :] = value
        for part in range(2 * RHS):
            total = red[pl.ds(part * SUB * SUB, SUB, stride=SUB), :]
            for d in range(1, SUB):
                total = total + red[pl.ds(part * SUB * SUB + d, SUB, stride=SUB), :]
            where = pl.ds(pl.multiple_of(part * DOF + cb * SUB, SUB), SUB)
            if add is not None:
                total = total + add[where, :]
            out[where, :] = total
        return carry

    lax.fori_loop(0, TILES, chunk, 0)


RED = pltpu.VMEM((2 * RHS * SUB * SUB, S), f32)


def local_dirs(n_x):
    dirs = ((0, (0,)), (1, (3,)), (2, (4,)))
    if n_x == 1:
        return dirs + ((3, (1, 2)),)
    return dirs + ((3, (1,)), (4, (2,)))


def local_apply(n_x, with_copy):
    def body(src, *refs):
        xs = [x[...] for x in refs[:n_x]]
        if n_x == 2:
            xs = swap_halves("xy", *xs)
        links, part = refs[n_x : n_x + 2]
        fields, red = refs[-2:]
        own = src[...]
        step = CZ * CT
        fields[0] = own.T
        fields[1] = jnp.concatenate([own[step:], own[:step]], axis=0).T
        fields[2] = jnp.concatenate([own[S - step :], own[: S - step]], axis=0).T
        for i, x in enumerate(xs):
            fields[3 + i] = x.T
        if with_copy:
            refs[n_x + 2][...] = fields[0]
        multiply(fields, links, local_dirs(n_x), red, part)

    outs = ((VEC, S),) * (2 if with_copy else 1)
    return call(body, outs, (pltpu.VMEM((3 + n_x, VEC, S), f32), RED))


REMOTE_DIRS = tuple((i, (5 + i,)) for i in range(4))


def gather_fields(src, za, zb, ta, tb, fields, pad):
    own = src[...].reshape(NY, CZ * CT, VEC)
    zp, zm = swap_halves("gz", za[...], zb[...])
    tp, tm = swap_halves("ta", ta[...], tb[...])
    zplus = jnp.concatenate([own[:, CT:], zp.reshape(NY, CT, VEC)], axis=1)
    fields[0] = zplus.reshape(S, VEC).T
    zminus = jnp.concatenate([zm.reshape(NY, CT, VEC), own[:, : (CZ - 1) * CT]], axis=1)
    fields[1] = zminus.reshape(S, VEC).T
    rows = S // CT
    for i in range(rows):
        pad[2 * i * CT : (2 * i + 1) * CT, :] = src[i * CT : (i + 1) * CT, :]
    pad[pl.ds(CT, rows, stride=2 * CT), :] = tp
    tplus = jnp.concatenate(
        [pad[2 * i * CT + 1 : (2 * i + 1) * CT + 1, :] for i in range(rows)], axis=0
    )
    fields[2] = tplus.T
    for i in range(rows):
        pad[(2 * i + 1) * CT : (2 * i + 2) * CT, :] = src[i * CT : (i + 1) * CT, :]
    pad[pl.ds(CT - 1, rows, stride=2 * CT), :] = tm
    tminus = jnp.concatenate(
        [pad[(2 * i + 1) * CT - 1 : (2 * i + 2) * CT - 1, :] for i in range(rows)], axis=0
    )
    fields[3] = tminus.T


REMOTE_SCRATCH = (pltpu.VMEM((4, VEC, S), f32), RED, pltpu.VMEM((2 * S, VEC), f32))


def first_body(src, za, zb, ta, tb, links, part, out_t, out, *refs):
    faces, (fields, red, pad) = refs[:4], refs[4:]
    gather_fields(src, za, zb, ta, tb, fields, pad)
    multiply(fields, links, REMOTE_DIRS, red, out_t, part)
    out[...] = out_t[...].T
    write_faces(out, *faces)


def halves(ref, r):
    top = 2 * r * DOF
    return ref[top : top + DOF, :], ref[top + DOF : top + 2 * DOF, :]


def column(values):
    return jnp.sum(values, axis=0, keepdims=True)


def square(u):
    return [column(u[0] * u[0] + u[1] * u[1])]


def inner(u, w):
    return [column(u[0] * w[0] + u[1] * w[1]), column(u[0] * w[1] - u[1] * w[0])]


TERMS = 9


def second_body(src, za, zb, ta, tb, links, part, first_t, zero_t, *refs):
    out_t, sums, fields, red, pad, table = refs
    gather_fields(src, za, zb, ta, tb, fields, pad)
    multiply(fields, links, REMOTE_DIRS, red, out_t, part)
    table[...] = jnp.zeros_like(table)
    for r in range(RHS):
        b, u, w = halves(zero_t, r), halves(first_t, r), halves(out_t, r)
        rows = square(b) + inner(b, u) + square(u) + inner(b, w) + inner(u, w) + square(w)
        for i, row in enumerate(rows):
            table[r * TERMS + i : r * TERMS + i + 1, :] = row
    total = column(table[...].T)
    sums[...] = jnp.broadcast_to(total[None], sums.shape)


def times(u, w):
    return (u[0] * w[0] - u[1] * w[1], u[0] * w[1] + u[1] * w[0])


def conj_times(u, w):
    return (u[0] * w[0] + u[1] * w[1], u[0] * w[1] - u[1] * w[0])


def plus(u, w):
    return (u[0] + w[0], u[1] + w[1])


def minus(u, w):
    return (u[0] - w[0], u[1] - w[1])


def scaled(s, u):
    return (s * u[0], s * u[1])


def norm2(u):
    return u[0] * u[0] + u[1] * u[1]


def coefficients(bb, bu, uu, bw, uw, ww):
    m = mass_shift
    inv = 1.0 / (bb + epsilon)
    tiny = epsilon * inv
    h00 = scaled(inv, (bu[0] + m * bb, bu[1]))
    q = (inv * bu[0] - m * tiny, inv * bu[1])
    pp = uu - 2.0 * conj_times(q, bu)[0] + norm2(q) * bb
    pp = jnp.maximum(pp, 0.0)
    s = pp * inv
    eta = s + epsilon
    bp = scaled(tiny, (bu[0] + m * bb, bu[1]))
    blp = minus(bw, times(q, bu))
    plp = minus(minus(uw, scaled(uu, q)), conj_times(q, bw))
    plp = plus(plp, scaled(norm2(q), bu))
    lplp = ww - 2.0 * conj_times(q, uw)[0] + norm2(q) * uu
    h01 = scaled(inv, plus(scaled(m, bp), blp))
    h11 = scaled(inv, (m * pp + plp[0], plp[1]))
    dp = inv * (m * m * pp + 2.0 * m * plp[0] + lplp)
    inv_eta = 1.0 / eta
    a00 = norm2(h00) + eta
    a01 = plus(conj_times(h00, h01), h11)
    cross = times(conj_times(h01, h11), bp)[0] * inv * inv_eta
    a11 = dp - norm2(h01) * tiny - norm2(h11) * (epsilon * inv_eta * inv_eta)
    a11 = a11 + 2.0 * cross + eta * epsilon
    inv00 = 1.0 / a00
    pivot = jnp.maximum(a11 - norm2(a01) * inv00, eta * epsilon)
    r0 = (h00[0], -h00[1])
    r1 = (h01[0], -h01[1])
    t = scaled(1.0 / pivot, minus(r1, scaled(inv00, conj_times(a01, r0))))
    y = scaled(inv00, minus(r0, times(a01, t)))
    return minus(y, times(t, q)), t


def final_body(sums, zero_t, first_t, second_t, sol, res, stage):
    total = jnp.sum(sums[...], axis=0)
    stage[...] = jnp.broadcast_to(total, stage.shape).T
    sol_rows = []
    res_rows = []
    for r in range(RHS):
        v = [stage[r * TERMS + i : r * TERMS + i + 1, :] for i in range(TERMS)]
        a, t = coefficients(v[0], (v[1], v[2]), v[3], (v[4], v[5]), (v[6], v[7]), v[8])
        b, u, w = halves(zero_t, r), halves(first_t, r), halves(second_t, r)
        x = plus(times(a, b), times(t, u))
        image = plus(scaled(mass_shift, x), plus(times(a, u), times(t, w)))
        left = minus(b, image)
        sol_rows += list(x)
        res_rows += list(left)
    sol[...] = jnp.concatenate(sol_rows, axis=0).T
    res[...] = jnp.concatenate(res_rows, axis=0).T


def exchange(value, axis, offset):
    n = lax.axis_size(axis)
    if n % 2:
        raise ValueError("odd axis " + axis)
    return lax.ppermute(
        value, axis, [(i, (i + 1 if (i - offset) % 2 == 0 else i - 1) % n) for i in range(n)]
    )


def halo(value, faces):
    za, zb, ta, tb = faces
    sent = {}
    plan = [("xa", value, "xy", 0)]
    if lax.axis_size("xy") > 2:
        plan.append(("xb", value, "xy", 1))
    plan += [("tb", tb, "ta", 1), ("zb", zb, "gz", 1), ("ta", ta, "ta", 0), ("za", za, "gz", 0)]
    for key, piece, axis, offset in plan:
        sent[key] = exchange(piece, axis, offset)
    xs = [sent[k] for k in ("xa", "xb") if k in sent]
    return xs, [sent[k] for k in ("za", "zb", "ta", "tb")]


def shards(right_side, link_blocks):
    b = right_side.reshape(S, VEC)
    links = link_blocks.reshape(link_blocks.shape[3:])
    links = pltpu.with_memory_space_constraint(links, pltpu.VMEM)
    n_x = 1 if lax.axis_size("xy") == 2 else 2
    devices = lax.axis_size("xy") * lax.axis_size("gz") * lax.axis_size("ta")

    faces = call(faces_body, FACES, (), FIRST_COST)(b)
    xs, edges = halo(b, faces)
    part, b_t = local_apply(n_x, True)(b, *xs, links)
    u_t, u, *faces = call(
        first_body, ((VEC, S), (S, VEC)) + FACES, REMOTE_SCRATCH
    )(b, *edges, links, part)
    xs, edges = halo(u, faces)
    (part,) = local_apply(n_x, False)(u, *xs, links)
    w_t, sums = call(
        second_body, ((VEC, S), (devices, 1, S)), REMOTE_SCRATCH + (pltpu.VMEM((S, S), f32),)
    )(u, *edges, links, part, u_t, b_t)
    sums = lax.all_to_all(sums, AXES, 0, 0)
    sol, res = call(final_body, ((S, VEC), (S, VEC)), (pltpu.VMEM((S, S), f32),))(
        sums, b_t, u_t, w_t
    )
    return sol.reshape(right_side.shape), res.reshape(right_side.shape)


def solution(mesh):
    return jax.shard_map(
        shards,
        mesh=mesh,
        in_specs=(
            P("xy", "gz", "ta", None, None),
            P("xy", "gz", "ta", None, None, None, None, None),
        ),
        out_specs=(P("xy", "gz", "ta", None, None), P("xy", "gz", "ta", None, None)),
        check_vma=False,
    )
```

profile of v0, /device:TPU:0, one launch (start us, length us, event | category | flops | bytes accessed | tf_op | source)
XLA Modules:
  0.0 36.5 jit_solution(17083673776846412494)
XLA Ops:
  0.6 0.0 slice-start
  0.6 0.0 slice-start.1
  0.7 0.0 slice-start.2
  0.7 0.6 %collective-permute-start.4 = (f32[128,128]{1,0:T(8,128)}, f32[128,128]{1,0:T(8,128)S(1)}, u32[]{:S(2)}, u32[]{:S(2)}) collective-permute-start(f32[128,128]{1,0:T(8,128)} %bitcast.10), channel_id=1, source_target_pairs={{0,16},{16,0},{1,17},{17,1},{2,18},{18,2},{3,19},{19,3},{4,20},{20... | collective-permute-start | bytes 196616 | tf_op jit(solution)/shard_map/ppermute | solution.py:287
  1.2 0.0 copy-start
  1.2 1.1 %copy-done = f32[1,1,1,128,128]{4,3,2,1,0:T(8,128)S(1)} copy-done((f32[1,1,1,128,128]{4,3,2,1,0:T(8,128)S(1)}, f32[1,1,1,128,128]{4,3,2,1,0:T(8,128)}, u32[]{:S(2)}) %copy-start) | copy-done | bytes 65560
  2.4 2.4 %collective-permute-start = (f32[64,128]{1,0:T(8,128)S(1)}, f32[64,128]{1,0:T(8,128)S(1)}, u32[]{:S(2)}, u32[]{:S(2)}) collective-permute-start(f32[64,128]{1,0:T(8,128)S(1)} %get-tuple-element.18), channel_id=1, source_target_pairs={{0,4},{4,0},{8,12},{12,8},{1,5},{5,1},{9,13},{13,9},{2,6},{6,2},{1... | collective-permute-start | bytes 98312 | tf_op jit(solution)/shard_map/ppermute | solution.py:287
  4.8 1.5 %collective-permute-start.1 = (f32[64,128]{1,0:T(8,128)S(1)}, f32[64,128]{1,0:T(8,128)S(1)}, u32[]{:S(2)}, u32[]{:S(2)}) collective-permute-start(f32[64,128]{1,0:T(8,128)S(1)} %get-tuple-element.19), channel_id=1, source_target_pairs={{0,12},{4,8},{8,4},{12,0},{1,13},{5,9},{9,5},{13,1},{2,14},{6,10},... | collective-permute-start | bytes 98312 | tf_op jit(solution)/shard_map/ppermute | solution.py:287
  6.3 1.6 %collective-permute-start.2 = (f32[16,128]{1,0:T(8,128)S(1)}, f32[16,128]{1,0:T(8,128)S(1)}, u32[]{:S(2)}, u32[]{:S(2)}) collective-permute-start(f32[16,128]{1,0:T(8,128)S(1)} %get-tuple-element.20), channel_id=1, source_target_pairs={{0,1},{1,0},{2,3},{3,2},{4,5},{5,4},{6,7},{7,6},{8,9},{9,8},{10,11... | collective-permute-start | bytes 24584 | tf_op jit(solution)/shard_map/ppermute | solution.py:287
  7.8 2.5 %collective-permute-start.3 = (f32[16,128]{1,0:T(8,128)S(1)}, f32[16,128]{1,0:T(8,128)S(1)}, u32[]{:S(2)}, u32[]{:S(2)}) collective-permute-start(f32[16,128]{1,0:T(8,128)S(1)} %get-tuple-element.21), channel_id=1, source_target_pairs={{0,3},{1,2},{2,1},{3,0},{4,7},{5,6},{6,5},{7,4},{8,11},{9,10},{10,... | collective-permute-start | bytes 24584 | tf_op jit(solution)/shard_map/ppermute | solution.py:287
  10.3 0.0 collective-permute-done.4.refs_0_
  10.3 0.0 slice-done
  10.3 0.0 slice-done.1
  10.3 0.0 slice-done.2
  10.4 1.4 %shard_map.42 = (f32[128,128]{1,0:T(8,128)S(1)}, f32[128,128]{1,0:T(8,128)S(1)}) custom-call(f32[128,128]{1,0:T(8,128)S(1)} %bitcast.12, f32[128,128]{1,0:T(8,128)S(1)} %collective-permute-done.4.refs_0_, f32[9,2,32,32,128]{4,3,2,1,0:T(8,128)S(1)} %bitcast.6), custom_call_target="tpu_custom_call" | custom-call | tf_op jit(solution)/shard_map/pallas_call | solution.py:314
  11.7 0.0 collective-permute-done.2.ta
  11.7 1.6 %collective-permute-done.3.tb = f32[16,128]{1,0:T(8,128)S(1)} collective-permute-done((f32[16,128]{1,0:T(8,128)S(1)}, f32[16,128]{1,0:T(8,128)S(1)}, u32[]{:S(2)}, u32[]{:S(2)}) %collective-permute-start.3) | collective-permute-done | bytes 8224 | tf_op jit(solution)/shard_map/ppermute | solution.py:287
  13.3 0.0 collective-permute-done.za
  13.3 0.0 collective-permute-done.1.zb
  13.3 1.5 %shard_map.43 = (f32[128,128]{1,0:T(8,128)S(1)}, f32[128,128]{1,0:T(8,128)S(1)}, f32[64,128]{1,0:T(8,128)S(1)}, f32[64,128]{1,0:T(8,128)S(1)}, f32[16,128]{1,0:T(8,128)S(1)}, /*index=5*/f32[16,128]{1,0:T(8,128)S(1)}) custom-call(f32[128,128]{1,0:T(8,128)S(1)} %bitcast.13, f32[64,128]{1,0:T(8,128)S(1)} %collective-permute-done.za, ...), custom_call_target="tpu_custom_call" | custom-call | tf_op jit(solution)/shard_map/pallas_call | solution.py:315
  14.8 0.1 collective-permute-start.9
  14.8 1.6 %collective-permute-start.5 = (f32[64,128]{1,0:T(8,128)S(1)}, f32[64,128]{1,0:T(8,128)S(1)}, u32[]{:S(2)}, u32[]{:S(2)}) collective-permute-start(f32[64,128]{1,0:T(8,128)S(1)} %get-tuple-element.24), channel_id=1, source_target_pairs={{0,4},{4,0},{8,12},{12,8},{1,5},{5,1},{9,13},{13,9},{2,6},{6,2},{1... | collective-permute-start | bytes 98312 | tf_op jit(solution)/shard_map/ppermute | solution.py:287
  16.4 0.5 %collective-permute-start.6 = (f32[64,128]{1,0:T(8,128)S(1)}, f32[64,128]{1,0:T(8,128)S(1)}, u32[]{:S(2)}, u32[]{:S(2)}) collective-permute-start(f32[64,128]{1,0:T(8,128)S(1)} %get-tuple-element.25), channel_id=1, source_target_pairs={{0,12},{4,8},{8,4},{12,0},{1,13},{5,9},{9,5},{13,1},{2,14},{6,10},... | collective-permute-start | bytes 98312 | tf_op jit(solution)/shard_map/ppermute | solution.py:287
  16.9 0.0 collective-permute-start.7
  16.9 2.5 %collective-permute-start.8 = (f32[16,128]{1,0:T(8,128)S(1)}, f32[16,128]{1,0:T(8,128)S(1)}, u32[]{:S(2)}, u32[]{:S(2)}) collective-permute-start(f32[16,128]{1,0:T(8,128)S(1)} %get-tuple-element.27), channel_id=1, source_target_pairs={{0,3},{1,2},{2,1},{3,0},{4,7},{5,6},{6,5},{7,4},{8,11},{9,10},{10,... | collective-permute-start | bytes 24584 | tf_op jit(solution)/shard_map/ppermute | solution.py:287
  19.4 0.0 collective-permute-done.9.refs_0_
  19.4 1.4 %shard_map.44.part = f32[128,128]{1,0:T(8,128)S(1)} custom-call(f32[128,128]{1,0:T(8,128)S(1)} %get-tuple-element.23.src, f32[128,128]{1,0:T(8,128)S(1)} %collective-permute-done.9.refs_0_, f32[9,2,32,32,128]{4,3,2,1,0:T(8,128)S(1)} %bitcast.8), custom_call_target="tpu_custom_call" | custom-call | tf_op jit(solution)/shard_map/pallas_call | solution.py:319
  20.7 0.0 collective-permute-done.7.ta
  20.7 1.6 %collective-permute-done.8.tb = f32[16,128]{1,0:T(8,128)S(1)} collective-permute-done((f32[16,128]{1,0:T(8,128)S(1)}, f32[16,128]{1,0:T(8,128)S(1)}, u32[]{:S(2)}, u32[]{:S(2)}) %collective-permute-start.8) | collective-permute-done | bytes 8224 | tf_op jit(solution)/shard_map/ppermute | solution.py:287
  22.3 0.0 collective-permute-done.5.za
  22.3 0.0 collective-permute-done.6.zb
  22.3 1.5 %shard_map.45 = (f32[128,128]{1,0:T(8,128)S(1)}, f32[32,1,128]{2,1,0:T(1,128)S(1)}) custom-call(f32[128,128]{1,0:T(8,128)S(1)} %get-tuple-element.23.src, f32[64,128]{1,0:T(8,128)S(1)} %collective-permute-done.5.za, f32[64,128]{1,0:T(8,128)S(1)} %collective-permute-done.6.zb, f32[16,128]{1,0:T(8,128)S(1)} %collective-permute-done.7.ta, ...), custom_call_target="tpu_custom_call" | custom-call | tf_op jit(solution)/shard_map/pallas_call | solution.py:320
  23.9 11.7 %all_to_all.5.sums = f32[32,1,128]{2,1,0:T(1,128)S(1)} all-to-all(f32[32,1,128]{2,1,0:T(1,128)S(1)} %get-tuple-element.30), channel_id=1, replica_groups=mesh['xy'=2,'gz'=4,'ta'=4] {'xy','gz','ta'}, dimensions={0} | all-to-all | bytes 32768 | tf_op jit(solution)/shard_map/all_to_all | solution.py:323
  35.5 0.9 %shard_map.46 = (f32[128,128]{1,0:T(8,128)}, f32[128,128]{1,0:T(8,128)}) custom-call(f32[32,1,128]{2,1,0:T(1,128)S(1)} %all_to_all.5.sums, f32[128,128]{1,0:T(8,128)S(1)} %get-tuple-element.29.zero_t, f32[128,128]{1,0:T(8,128)S(1)} %get-tuple-element.28.first_t, f32[128,128]{1,0:T(8,128)S(1)} %get-tuple-element.31.second_t), custom_call_target="tpu_custom_call" | custom-call | tf_op jit(solution)/shard_map/pallas_call | solution.py:324
  (2 shorter events, 0.0 us)
Async XLA Ops:
  0.6 9.7 %slice-start = ((s8[9437184]{0:T(1024)(128)(4,1)}), s8[4194304]{0:T(1024)(128)(4,1)S(1)}, s32[]{:S(2)}) async-start(s8[9437184]{0:T(1024)(128)(4,1)} %bitcast.4), calls=%async_computation.1 | async-start | bytes 8388608
  0.6 9.7 %slice-start.1 = ((s8[9437184]{0:T(1024)(128)(4,1)}), s8[4194304]{0:T(1024)(128)(4,1)S(1)}, s32[]{:S(2)}) async-start(s8[9437184]{0:T(1024)(128)(4,1)} %bitcast.4), calls=%async_computation.2 | async-start | bytes 8388608
  0.7 9.7 %slice-start.2 = ((s8[9437184]{0:T(1024)(128)(4,1)}), s8[1048576]{0:T(1024)(128)(4,1)S(1)}, s32[]{:S(2)}) async-start(s8[9437184]{0:T(1024)(128)(4,1)} %bitcast.4), calls=%async_computation.3 | async-start | bytes 2097152
  0.7 9.7 %collective-permute-start.4 = (f32[128,128]{1,0:T(8,128)}, f32[128,128]{1,0:T(8,128)S(1)}, u32[]{:S(2)}, u32[]{:S(2)}) collective-permute-start(f32[128,128]{1,0:T(8,128)} %bitcast.10), channel_id=1, source_target_pairs={{0,16},{16,0},{1,17},{17,1},{2,18},{18,2},{3,19},{19,3},{4,20},{20... | collective-permute-start | bytes 196616 | tf_op jit(solution)/shard_map/ppermute | solution.py:287
  1.2 1.1 %copy-start = (f32[1,1,1,128,128]{4,3,2,1,0:T(8,128)S(1)}, f32[1,1,1,128,128]{4,3,2,1,0:T(8,128)}, u32[]{:S(2)}) copy-start(f32[1,1,1,128,128]{4,3,2,1,0:T(8,128)} %param.2) | copy-start | bytes 196612
  2.4 10.9 %collective-permute-start = (f32[64,128]{1,0:T(8,128)S(1)}, f32[64,128]{1,0:T(8,128)S(1)}, u32[]{:S(2)}, u32[]{:S(2)}) collective-permute-start(f32[64,128]{1,0:T(8,128)S(1)} %get-tuple-element.18), channel_id=1, source_target_pairs={{0,4},{4,0},{8,12},{12,8},{1,5},{5,1},{9,13},{13,9},{2,6},{6,2},{1... | collective-permute-start | bytes 98312 | tf_op jit(solution)/shard_map/ppermute | solution.py:287
  4.8 8.5 %collective-permute-start.1 = (f32[64,128]{1,0:T(8,128)S(1)}, f32[64,128]{1,0:T(8,128)S(1)}, u32[]{:S(2)}, u32[]{:S(2)}) collective-permute-start(f32[64,128]{1,0:T(8,128)S(1)} %get-tuple-element.19), channel_id=1, source_target_pairs={{0,12},{4,8},{8,4},{12,0},{1,13},{5,9},{9,5},{13,1},{2,14},{6,10},... | collective-permute-start | bytes 98312 | tf_op jit(solution)/shard_map/ppermute | solution.py:287
  6.3 5.5 %collective-permute-start.2 = (f32[16,128]{1,0:T(8,128)S(1)}, f32[16,128]{1,0:T(8,128)S(1)}, u32[]{:S(2)}, u32[]{:S(2)}) collective-permute-start(f32[16,128]{1,0:T(8,128)S(1)} %get-tuple-element.20), channel_id=1, source_target_pairs={{0,1},{1,0},{2,3},{3,2},{4,5},{5,4},{6,7},{7,6},{8,9},{9,8},{10,11... | collective-permute-start | bytes 24584 | tf_op jit(solution)/shard_map/ppermute | solution.py:287
  7.8 5.4 %collective-permute-start.3 = (f32[16,128]{1,0:T(8,128)S(1)}, f32[16,128]{1,0:T(8,128)S(1)}, u32[]{:S(2)}, u32[]{:S(2)}) collective-permute-start(f32[16,128]{1,0:T(8,128)S(1)} %get-tuple-element.21), channel_id=1, source_target_pairs={{0,3},{1,2},{2,1},{3,0},{4,7},{5,6},{6,5},{7,4},{8,11},{9,10},{10,... | collective-permute-start | bytes 24584 | tf_op jit(solution)/shard_map/ppermute | solution.py:287
  14.8 4.6 %collective-permute-start.9 = (f32[128,128]{1,0:T(8,128)S(1)}, f32[128,128]{1,0:T(8,128)S(1)}, u32[]{:S(2)}, u32[]{:S(2)}) collective-permute-start(f32[128,128]{1,0:T(8,128)S(1)} %get-tuple-element.23.src), channel_id=1, source_target_pairs={{0,16},{16,0},{1,17},{17,1},{2,18},{18,2},{3,19},{19,3},{4,20},{20... | collective-permute-start | bytes 196616 | tf_op jit(solution)/shard_map/ppermute | solution.py:287
  14.8 7.5 %collective-permute-start.5 = (f32[64,128]{1,0:T(8,128)S(1)}, f32[64,128]{1,0:T(8,128)S(1)}, u32[]{:S(2)}, u32[]{:S(2)}) collective-permute-start(f32[64,128]{1,0:T(8,128)S(1)} %get-tuple-element.24), channel_id=1, source_target_pairs={{0,4},{4,0},{8,12},{12,8},{1,5},{5,1},{9,13},{13,9},{2,6},{6,2},{1... | collective-permute-start | bytes 98312 | tf_op jit(solution)/shard_map/ppermute | solution.py:287
  16.4 5.9 %collective-permute-start.6 = (f32[64,128]{1,0:T(8,128)S(1)}, f32[64,128]{1,0:T(8,128)S(1)}, u32[]{:S(2)}, u32[]{:S(2)}) collective-permute-start(f32[64,128]{1,0:T(8,128)S(1)} %get-tuple-element.25), channel_id=1, source_target_pairs={{0,12},{4,8},{8,4},{12,0},{1,13},{5,9},{9,5},{13,1},{2,14},{6,10},... | collective-permute-start | bytes 98312 | tf_op jit(solution)/shard_map/ppermute | solution.py:287
  16.9 3.9 %collective-permute-start.7 = (f32[16,128]{1,0:T(8,128)S(1)}, f32[16,128]{1,0:T(8,128)S(1)}, u32[]{:S(2)}, u32[]{:S(2)}) collective-permute-start(f32[16,128]{1,0:T(8,128)S(1)} %get-tuple-element.26), channel_id=1, source_target_pairs={{0,1},{1,0},{2,3},{3,2},{4,5},{5,4},{6,7},{7,6},{8,9},{9,8},{10,11... | collective-permute-start | bytes 24584 | tf_op jit(solution)/shard_map/ppermute | solution.py:287
  16.9 5.4 %collective-permute-start.8 = (f32[16,128]{1,0:T(8,128)S(1)}, f32[16,128]{1,0:T(8,128)S(1)}, u32[]{:S(2)}, u32[]{:S(2)}) collective-permute-start(f32[16,128]{1,0:T(8,128)S(1)} %get-tuple-element.27), channel_id=1, source_target_pairs={{0,3},{1,2},{2,1},{3,0},{4,7},{5,6},{6,5},{7,4},{8,11},{9,10},{10,... | collective-permute-start | bytes 24584 | tf_op jit(solution)/shard_map/ppermute | solution.py:287
where the time goes:
time: 36.6 us; the launch traced here: 36.5 us
  starting transfers between devices  13.1 us (36%)
  blocking collectives  11.7 us (32%)
  Pallas kernels  6.61 us (18%)
  waiting for transfers between devices  3.18 us (9%)
  local copies, waits for them, and re-layouts  1.14 us (3%)
  between operations  0.74 us (2%)
    ppermute x10, starting transfers between devices, exchange(): lax.ppermute(value, axis, [(i, (i + 1 if (i - offset) % 2 == 0 else i - 1...  13.1 us
    all_to_all x1, blocking collectives, shards(): sums = lax.all_to_all(sums, AXES, 0, 0)  11.7 us
    ppermute x10, waiting for transfers between devices, exchange(): lax.ppermute(value, axis, [(i, (i + 1 if (i - offset) % 2 == 0 else i - 1...  3.18 us
    pallas_call x1, Pallas kernels, shards(): call(second_body, ((VEC, S), (devices, 1, S)), REMOTE_SCRATCH + (pltpu.VM...  1.51 us
    pallas_call x1, Pallas kernels, shards(): call(first_body, ((VEC, S), (S, VEC)) + FACES, REMOTE_SCRATCH)  1.45 us
    pallas_call x1, Pallas kernels, shards(): part, b_t = local_apply(n_x, True)(b, *xs, links)  1.36 us
    pallas_call x1, Pallas kernels, shards(): part, = local_apply(n_x, False)(u, *xs, links)  1.36 us
    unnamed x8, local copies, waits for them, and re-layouts  1.14 us
  transfers between devices with their start and end apart: 10, of which 2 were waited for; matrix products, arithmetic and copies ran while one was open for 0% of the time, Pallas kernels for 7%

commit v1 on v0

--- a/solution.py
+++ b/solution.py
@@ -21,6 +21,7 @@
 mass_shift = 4.0
 epsilon = 1e-06
 f32 = jnp.float32
+ORDER = ("tb", "x", "zb", "ta", "za")
 FIRST_COST = 20_000_000_000
 
 VMEM_SPEC = pl.BlockSpec(memory_space=pltpu.VMEM)
@@ -103,14 +104,45 @@
 RED = pltpu.VMEM((2 * RHS * SUB * SUB, S), f32)
 
 
-def local_dirs(n_x):
-    dirs = ((0, (0,)), (1, (3,)), (2, (4,)))
-    if n_x == 1:
-        return dirs + ((3, (1, 2)),)
-    return dirs + ((3, (1,)), (4, (2,)))
-
-
-def local_apply(n_x, with_copy):
+def assemble_z(own, edge, plus):
+    blocks = own.reshape(NY, CZ * CT, VEC)
+    edge = edge.reshape(NY, CT, VEC)
+    up = jnp.concatenate([blocks[:, CT:], edge], axis=1)
+    down = jnp.concatenate([edge, blocks[:, : (CZ - 1) * CT]], axis=1)
+    return jnp.where(plus, up, down).reshape(S, VEC).T
+
+
+def assemble_t(own, edge, plus, pad):
+    rows = S // CT
+    step = 3 * CT
+    for i in range(rows):
+        pad[i * step + CT : i * step + 2 * CT, :] = own[i * CT : (i + 1) * CT, :]
+    pad[pl.ds(CT - 1, rows, stride=step), :] = edge
+    pad[pl.ds(2 * CT, rows, stride=step), :] = edge
+    pieces = []
+    for i in range(rows):
+        up = pad[i * step + CT + 1 : i * step + 2 * CT + 1, :]
+        down = pad[i * step + CT - 1 : i * step + 2 * CT - 1, :]
+        pieces.append(jnp.where(plus, up, down))
+    return jnp.concatenate(pieces, axis=0).T
+
+
+PAD = pltpu.VMEM((3 * S, VEC), f32)
+
+
+def edge_fields(own, z_edge, t_edge, which, fields, at, pad):
+    dirs = []
+    for k, axis in enumerate(("gz", "ta")):
+        down = (lax.axis_index(axis) + which) % 2
+        if axis == "gz":
+            fields[at] = assemble_z(own, z_edge, down == 0)
+        else:
+            fields[at + 1] = assemble_t(own, t_edge, down == 0, pad)
+        dirs.append((at + k, (5 + 2 * k + down,)))
+    return tuple(dirs)
+
+
+def local_part(n_x, with_copy):
     def body(src, *refs):
         xs = [x[...] for x in refs[:n_x]]
         if n_x == 2:
@@ -126,47 +158,33 @@
             fields[3 + i] = x.T
         if with_copy:
             refs[n_x + 2][...] = fields[0]
-        multiply(fields, links, local_dirs(n_x), red, part)
+        dirs = ((0, (0,)), (1, (3,)), (2, (4,)))
+        dirs += ((3, (1, 2)),) if n_x == 1 else ((3, (1,)), (4, (2,)))
+        multiply(fields, links, dirs, red, part)
 
     outs = ((VEC, S),) * (2 if with_copy else 1)
     return call(body, outs, (pltpu.VMEM((3 + n_x, VEC, S), f32), RED))
 
 
-REMOTE_DIRS = tuple((i, (5 + i,)) for i in range(4))
-
-
-def gather_fields(src, za, zb, ta, tb, fields, pad):
-    own = src[...].reshape(NY, CZ * CT, VEC)
-    zp, zm = swap_halves("gz", za[...], zb[...])
-    tp, tm = swap_halves("ta", ta[...], tb[...])
-    zplus = jnp.concatenate([own[:, CT:], zp.reshape(NY, CT, VEC)], axis=1)
-    fields[0] = zplus.reshape(S, VEC).T
-    zminus = jnp.concatenate([zm.reshape(NY, CT, VEC), own[:, : (CZ - 1) * CT]], axis=1)
-    fields[1] = zminus.reshape(S, VEC).T
-    rows = S // CT
-    for i in range(rows):
-        pad[2 * i * CT : (2 * i + 1) * CT, :] = src[i * CT : (i + 1) * CT, :]
-    pad[pl.ds(CT, rows, stride=2 * CT), :] = tp
-    tplus = jnp.concatenate(
-        [pad[2 * i * CT + 1 : (2 * i + 1) * CT + 1, :] for i in range(rows)], axis=0
-    )
-    fields[2] = tplus.T
-    for i in range(rows):
-        pad[(2 * i + 1) * CT : (2 * i + 2) * CT, :] = src[i * CT : (i + 1) * CT, :]
-    pad[pl.ds(CT - 1, rows, stride=2 * CT), :] = tm
-    tminus = jnp.concatenate(
-        [pad[(2 * i + 1) * CT - 1 : (2 * i + 2) * CT - 1, :] for i in range(rows)], axis=0
-    )
-    fields[3] = tminus.T
-
-
-REMOTE_SCRATCH = (pltpu.VMEM((4, VEC, S), f32), RED, pltpu.VMEM((2 * S, VEC), f32))
-
-
-def first_body(src, za, zb, ta, tb, links, part, out_t, out, *refs):
-    faces, (fields, red, pad) = refs[:4], refs[4:]
-    gather_fields(src, za, zb, ta, tb, fields, pad)
-    multiply(fields, links, REMOTE_DIRS, red, out_t, part)
+LAST_SCRATCH = (pltpu.VMEM((2, VEC, S), f32), RED, PAD)
+
+
+def edge_part(which, src, ze, te, links, part, out_t, fields, red, pad):
+    dirs = edge_fields(src[...], ze[...], te[...], which, fields, 0, pad)
+    multiply(fields, links, dirs, red, out_t, part)
+
+
+def edge_body(*refs):
+    edge_part(1, *refs)
+
+
+def add_edges(*args):
+    return call(edge_body, ((VEC, S),), LAST_SCRATCH)(*args)[0]
+
+
+def first_body(src, za, ta, links, part, out_t, out, *refs):
+    faces, scratch = refs[:4], refs[4:]
+    edge_part(0, src, za, ta, links, part, out_t, *scratch)
     out[...] = out_t[...].T
     write_faces(out, *faces)
 
@@ -191,10 +209,9 @@
 TERMS = 9
 
 
-def second_body(src, za, zb, ta, tb, links, part, first_t, zero_t, *refs):
-    out_t, sums, fields, red, pad, table = refs
-    gather_fields(src, za, zb, ta, tb, fields, pad)
-    multiply(fields, links, REMOTE_DIRS, red, out_t, part)
+def second_body(src, za, ta, links, part, first_t, zero_t, out_t, sums, *refs):
+    table, scratch = refs[-1], refs[:-1]
+    edge_part(0, src, za, ta, links, part, out_t, *scratch)
     table[...] = jnp.zeros_like(table)
     for r in range(RHS):
         b, u, w = halves(zero_t, r), halves(first_t, r), halves(out_t, r)
@@ -292,14 +309,20 @@
 def halo(value, faces):
     za, zb, ta, tb = faces
     sent = {}
-    plan = [("xa", value, "xy", 0)]
+    plan = {
+        "tb": [("tb", tb, "ta", 1)],
+        "zb": [("zb", zb, "gz", 1)],
+        "za": [("za", za, "gz", 0)],
+        "ta": [("ta", ta, "ta", 0)],
+        "x": [("xa", value, "xy", 0)],
+    }
     if lax.axis_size("xy") > 2:
-        plan.append(("xb", value, "xy", 1))
-    plan += [("tb", tb, "ta", 1), ("zb", zb, "gz", 1), ("ta", ta, "ta", 0), ("za", za, "gz", 0)]
+        plan["x"].append(("xb", value, "xy", 1))
+    plan = [entry for key in ORDER for entry in plan[key]]
     for key, piece, axis, offset in plan:
         sent[key] = exchange(piece, axis, offset)
     xs = [sent[k] for k in ("xa", "xb") if k in sent]
-    return xs, [sent[k] for k in ("za", "zb", "ta", "tb")]
+    return xs, [sent["zb"], sent["tb"]], [sent["za"], sent["ta"]]
 
 
 def shards(right_side, link_blocks):
@@ -310,16 +333,20 @@
     devices = lax.axis_size("xy") * lax.axis_size("gz") * lax.axis_size("ta")
 
     faces = call(faces_body, FACES, (), FIRST_COST)(b)
-    xs, edges = halo(b, faces)
-    part, b_t = local_apply(n_x, True)(b, *xs, links)
+    xs, early, late = halo(b, faces)
+    part, b_t = local_part(n_x, True)(b, *xs, links)
+    part = add_edges(b, *early, links, part)
     u_t, u, *faces = call(
-        first_body, ((VEC, S), (S, VEC)) + FACES, REMOTE_SCRATCH
-    )(b, *edges, links, part)
-    xs, edges = halo(u, faces)
-    (part,) = local_apply(n_x, False)(u, *xs, links)
+        first_body, ((VEC, S), (S, VEC)) + FACES, LAST_SCRATCH
+    )(b, *late, links, part)
+    xs, early, late = halo(u, faces)
+    (part,) = local_part(n_x, False)(u, *xs, links)
+    part = add_edges(u, *early, links, part)
     w_t, sums = call(
-        second_body, ((VEC, S), (devices, 1, S)), REMOTE_SCRATCH + (pltpu.VMEM((S, S), f32),)
-    )(u, *edges, links, part, u_t, b_t)
+        second_body,
+        ((VEC, S), (devices, 1, S)),
+        LAST_SCRATCH + (pltpu.VMEM((S, S), f32),),
+    )(u, *late, links, part, u_t, b_t)
     sums = lax.all_to_all(sums, AXES, 0, 0)
     sol, res = call(final_body, ((S, VEC), (S, VEC)), (pltpu.VMEM((S, S), f32),))(
         sums, b_t, u_t, w_t

time: 36.6 us -> 36.6 us (level)
  Pallas kernels: 6.61 us -> 7 us
    pallas_call x4 -> x6, Pallas kernels: 5.68 us -> 6.07 us  [the longest x2 1.54 us: add_edges(): return call(edge_body, ((VEC, S),), LAST_SCRATCH)(*args)[0]]
  transfers between devices with their start and end apart: 10 -> 10, of which waited for: 2 -> 3; matrix products, arithmetic and copies ran while one was open for 0% -> 0% of each run, Pallas kernels for 7% -> 12%
where the time goes in v1:
time: 36.6 us; the launch traced here: 36.4 us
  starting transfers between devices  12.8 us (35%)
  blocking collectives  11.8 us (32%)
  Pallas kernels  7 us (19%)
  waiting for transfers between devices  2.97 us (8%)
  local copies, waits for them, and re-layouts  1.14 us (3%)
  between operations  0.75 us (2%)
    ppermute x10, starting transfers between devices, exchange(): lax.ppermute(value, axis, [(i, (i + 1 if (i - offset) % 2 == 0 else i - 1...  12.8 us
    all_to_all x1, blocking collectives, shards(): sums = lax.all_to_all(sums, AXES, 0, 0)  11.8 us
    ppermute x10, waiting for transfers between devices, exchange(): lax.ppermute(value, axis, [(i, (i + 1 if (i - offset) % 2 == 0 else i - 1...  2.97 us
    pallas_call x2, Pallas kernels, add_edges(): return call(edge_body, ((VEC, S),), LAST_SCRATCH)(*args)[0]  1.54 us
    pallas_call x1, Pallas kernels, shards(): part, b_t = local_part(n_x, True)(b, *xs, links)  1.36 us
    pallas_call x1, Pallas kernels, shards(): part, = local_part(n_x, False)(u, *xs, links)  1.36 us
    unnamed x8, local copies, waits for them, and re-layouts  1.14 us
    pallas_call x1, Pallas kernels, shards(): call(second_body, ((VEC, S), (devices, 1, S)), LAST_SCRATCH + (pltpu.VMEM...  0.94 us
  transfers between devices with their start and end apart: 10, of which 3 were waited for; matrix products, arithmetic and copies ran while one was open for 0% of the time, Pallas kernels for 12%

profile of v1, /device:TPU:0, one launch (start us, length us, event | category | flops | bytes accessed | tf_op | source)
XLA Modules:
  0.0 36.4 jit_solution(18405321119912422130)
XLA Ops:
  0.6 0.0 slice-start
  0.6 0.0 slice-start.1
  0.7 0.0 slice-start.2
  0.7 0.6 %collective-permute-start.4 = (f32[128,128]{1,0:T(8,128)}, f32[128,128]{1,0:T(8,128)S(1)}, u32[]{:S(2)}, u32[]{:S(2)}) collective-permute-start(f32[128,128]{1,0:T(8,128)} %bitcast.12), channel_id=1, source_target_pairs={{0,16},{16,0},{1,17},{17,1},{2,18},{18,2},{3,19},{19,3},{4,20},{20... | collective-permute-start | bytes 196616 | tf_op jit(solution)/shard_map/ppermute | solution.py:304
  1.2 0.0 copy-start
  1.2 1.1 %copy-done = f32[1,1,1,128,128]{4,3,2,1,0:T(8,128)S(1)} copy-done((f32[1,1,1,128,128]{4,3,2,1,0:T(8,128)S(1)}, f32[1,1,1,128,128]{4,3,2,1,0:T(8,128)}, u32[]{:S(2)}) %copy-start) | copy-done | bytes 65560
  2.4 3.4 %collective-permute-start.2 = (f32[64,128]{1,0:T(8,128)S(1)}, f32[64,128]{1,0:T(8,128)S(1)}, u32[]{:S(2)}, u32[]{:S(2)}) collective-permute-start(f32[64,128]{1,0:T(8,128)S(1)} %get-tuple-element.20), channel_id=1, source_target_pairs={{0,12},{4,8},{8,4},{12,0},{1,13},{5,9},{9,5},{13,1},{2,14},{6,10},... | collective-permute-start | bytes 98312 | tf_op jit(solution)/shard_map/ppermute | solution.py:304
  5.7 0.5 %collective-permute-start = (f32[64,128]{1,0:T(8,128)S(1)}, f32[64,128]{1,0:T(8,128)S(1)}, u32[]{:S(2)}, u32[]{:S(2)}) collective-permute-start(f32[64,128]{1,0:T(8,128)S(1)} %get-tuple-element.18), channel_id=1, source_target_pairs={{0,4},{4,0},{8,12},{12,8},{1,5},{5,1},{9,13},{13,9},{2,6},{6,2},{1... | collective-permute-start | bytes 98312 | tf_op jit(solution)/shard_map/ppermute | solution.py:304
  6.3 3.6 %collective-permute-start.3 = (f32[16,128]{1,0:T(8,128)S(1)}, f32[16,128]{1,0:T(8,128)S(1)}, u32[]{:S(2)}, u32[]{:S(2)}) collective-permute-start(f32[16,128]{1,0:T(8,128)S(1)} %get-tuple-element.21), channel_id=1, source_target_pairs={{0,3},{1,2},{2,1},{3,0},{4,7},{5,6},{6,5},{7,4},{8,11},{9,10},{10,... | collective-permute-start | bytes 24584 | tf_op jit(solution)/shard_map/ppermute | solution.py:304
  9.9 0.0 collective-permute-start.1
  9.9 0.0 collective-permute-done.4.refs_0_
  9.9 0.0 slice-done
  9.9 0.0 slice-done.1
  9.9 0.0 slice-done.2
  9.9 1.4 %shard_map.42 = (f32[128,128]{1,0:T(8,128)S(1)}, f32[128,128]{1,0:T(8,128)S(1)}) custom-call(f32[128,128]{1,0:T(8,128)S(1)} %bitcast.14, f32[128,128]{1,0:T(8,128)S(1)} %collective-permute-done.4.refs_0_, f32[9,2,32,32,128]{4,3,2,1,0:T(8,128)S(1)} %bitcast.6), custom_call_target="tpu_custom_call" | custom-call | tf_op jit(solution)/shard_map/pallas_call | solution.py:337
  11.3 0.4 %collective-permute-done.3.refs_2_ = f32[16,128]{1,0:T(8,128)S(1)} collective-permute-done((f32[16,128]{1,0:T(8,128)S(1)}, f32[16,128]{1,0:T(8,128)S(1)}, u32[]{:S(2)}, u32[]{:S(2)}) %collective-permute-start.3) | collective-permute-done | bytes 8224 | tf_op jit(solution)/shard_map/ppermute | solution.py:304
  11.7 0.0 collective-permute-done.2.refs_1_
  11.7 0.8 %shard_map.43.part = f32[128,128]{1,0:T(8,128)S(1)} custom-call(f32[128,128]{1,0:T(8,128)S(1)} %bitcast.15, f32[64,128]{1,0:T(8,128)S(1)} %collective-permute-done.2.refs_1_, f32[16,128]{1,0:T(8,128)S(1)} %collective-permute-done.3.refs_2_, f32[9,2,32,32,128]{4,3,2,1,0:T(8,128)S(1)} %bitcast.7, f32[128,128]{1,0:T(8,128)S(1)} %get-tuple-element.22.refs_4_), custom_call_target="tpu_custom_call" | custom-call | tf_op jit(solution)/shard_map/pallas_call | solution.py:182
  12.5 1.0 %collective-permute-done.1.ta = f32[16,128]{1,0:T(8,128)S(1)} collective-permute-done((f32[16,128]{1,0:T(8,128)S(1)}, f32[16,128]{1,0:T(8,128)S(1)}, u32[]{:S(2)}, u32[]{:S(2)}) %collective-permute-start.1) | collective-permute-done | bytes 8224 | tf_op jit(solution)/shard_map/ppermute | solution.py:304
  13.5 0.0 collective-permute-done.za
  13.5 0.9 %shard_map.44 = (f32[128,128]{1,0:T(8,128)S(1)}, f32[128,128]{1,0:T(8,128)S(1)}, f32[64,128]{1,0:T(8,128)S(1)}, f32[64,128]{1,0:T(8,128)S(1)}, f32[16,128]{1,0:T(8,128)S(1)}, /*index=5*/f32[16,128]{1,0:T(8,128)S(1)}) custom-call(f32[128,128]{1,0:T(8,128)S(1)} %bitcast.16, f32[64,128]{1,0:T(8,128)S(1)} %collective-permute-done.za, ...), custom_call_target="tpu_custom_call" | custom-call | tf_op jit(solution)/shard_map/pallas_call | solution.py:339
  14.4 0.1 collective-permute-start.9
  14.5 1.5 %collective-permute-start.7 = (f32[64,128]{1,0:T(8,128)S(1)}, f32[64,128]{1,0:T(8,128)S(1)}, u32[]{:S(2)}, u32[]{:S(2)}) collective-permute-start(f32[64,128]{1,0:T(8,128)S(1)} %get-tuple-element.26), channel_id=1, source_target_pairs={{0,12},{4,8},{8,4},{12,0},{1,13},{5,9},{9,5},{13,1},{2,14},{6,10},... | collective-permute-start | bytes 98312 | tf_op jit(solution)/shard_map/ppermute | solution.py:304
  16.0 0.5 %collective-permute-start.5 = (f32[64,128]{1,0:T(8,128)S(1)}, f32[64,128]{1,0:T(8,128)S(1)}, u32[]{:S(2)}, u32[]{:S(2)}) collective-permute-start(f32[64,128]{1,0:T(8,128)S(1)} %get-tuple-element.24), channel_id=1, source_target_pairs={{0,4},{4,0},{8,12},{12,8},{1,5},{5,1},{9,13},{13,9},{2,6},{6,2},{1... | collective-permute-start | bytes 98312 | tf_op jit(solution)/shard_map/ppermute | solution.py:304
  16.5 2.6 %collective-permute-start.8 = (f32[16,128]{1,0:T(8,128)S(1)}, f32[16,128]{1,0:T(8,128)S(1)}, u32[]{:S(2)}, u32[]{:S(2)}) collective-permute-start(f32[16,128]{1,0:T(8,128)S(1)} %get-tuple-element.27), channel_id=1, source_target_pairs={{0,3},{1,2},{2,1},{3,0},{4,7},{5,6},{6,5},{7,4},{8,11},{9,10},{10,... | collective-permute-start | bytes 24584 | tf_op jit(solution)/shard_map/ppermute | solution.py:304
  19.1 0.0 collective-permute-start.6
  19.1 0.0 collective-permute-done.9.refs_0_
  19.1 1.4 %shard_map.45.refs_4_ = f32[128,128]{1,0:T(8,128)S(1)} custom-call(f32[128,128]{1,0:T(8,128)S(1)} %get-tuple-element.23.src.refs_0_, f32[128,128]{1,0:T(8,128)S(1)} %collective-permute-done.9.refs_0_, f32[9,2,32,32,128]{4,3,2,1,0:T(8,128)S(1)} %bitcast.9), custom_call_target="tpu_custom_call" | custom-call | tf_op jit(solution)/shard_map/pallas_call | solution.py:343
  20.5 1.5 %collective-permute-done.8.refs_2_ = f32[16,128]{1,0:T(8,128)S(1)} collective-permute-done((f32[16,128]{1,0:T(8,128)S(1)}, f32[16,128]{1,0:T(8,128)S(1)}, u32[]{:S(2)}, u32[]{:S(2)}) %collective-permute-start.8) | collective-permute-done | bytes 8224 | tf_op jit(solution)/shard_map/ppermute | solution.py:304
  22.0 0.0 collective-permute-done.7.refs_1_
  22.0 0.8 %shard_map.46.part = f32[128,128]{1,0:T(8,128)S(1)} custom-call(f32[128,128]{1,0:T(8,128)S(1)} %get-tuple-element.23.src.refs_0_, f32[64,128]{1,0:T(8,128)S(1)} %collective-permute-done.7.refs_1_, f32[16,128]{1,0:T(8,128)S(1)} %collective-permute-done.8.refs_2_, f32[9,2,32,32,128]{4,3,2,1,0:T(8,128)S(1)} %bitcast.10, f32[128,128]{1,0:T(8,128)S(1)} %shard_map.45.refs_4_), custom_call_target="tpu_custom_call" | custom-call | tf_op jit(solution)/shard_map/pallas_call | solution.py:182
  22.7 0.0 collective-permute-done.6.ta
  22.8 0.0 collective-permute-done.5.za
  22.8 0.9 %shard_map.47 = (f32[128,128]{1,0:T(8,128)S(1)}, f32[32,1,128]{2,1,0:T(1,128)S(1)}) custom-call(f32[128,128]{1,0:T(8,128)S(1)} %get-tuple-element.23.src.refs_0_, f32[64,128]{1,0:T(8,128)S(1)} %collective-permute-done.5.za, f32[16,128]{1,0:T(8,128)S(1)} %collective-permute-done.6.ta, f32[9,2,32,32,128]{4,3,2,1,0:T(8,128)S(1)} %bitcast.11, ...), custom_call_target="tpu_custom_call" | custom-call | tf_op jit(solution)/shard_map/pallas_call | solution.py:345
  23.7 11.8 %all_to_all.5.sums = f32[32,1,128]{2,1,0:T(1,128)S(1)} all-to-all(f32[32,1,128]{2,1,0:T(1,128)S(1)} %get-tuple-element.30), channel_id=1, replica_groups=mesh['xy'=2,'gz'=4,'ta'=4] {'xy','gz','ta'}, dimensions={0} | all-to-all | bytes 32768 | tf_op jit(solution)/shard_map/all_to_all | solution.py:350
  35.5 0.9 %shard_map.48 = (f32[128,128]{1,0:T(8,128)}, f32[128,128]{1,0:T(8,128)}) custom-call(f32[32,1,128]{2,1,0:T(1,128)S(1)} %all_to_all.5.sums, f32[128,128]{1,0:T(8,128)S(1)} %get-tuple-element.29.zero_t, f32[128,128]{1,0:T(8,128)S(1)} %get-tuple-element.28.first_t, f32[128,128]{1,0:T(8,128)S(1)} %get-tuple-element.31.second_t), custom_call_target="tpu_custom_call" | custom-call | tf_op jit(solution)/shard_map/pallas_call | solution.py:351
  (2 shorter events, 0.0 us)
Async XLA Ops:
  0.6 9.3 %slice-start = ((s8[9437184]{0:T(1024)(128)(4,1)}), s8[4194304]{0:T(1024)(128)(4,1)S(1)}, s32[]{:S(2)}) async-start(s8[9437184]{0:T(1024)(128)(4,1)} %bitcast.4), calls=%async_computation.1 | async-start | bytes 8388608
  0.6 9.2 %slice-start.1 = ((s8[9437184]{0:T(1024)(128)(4,1)}), s8[4194304]{0:T(1024)(128)(4,1)S(1)}, s32[]{:S(2)}) async-start(s8[9437184]{0:T(1024)(128)(4,1)} %bitcast.4), calls=%async_computation.2 | async-start | bytes 8388608
  0.7 9.2 %slice-start.2 = ((s8[9437184]{0:T(1024)(128)(4,1)}), s8[1048576]{0:T(1024)(128)(4,1)S(1)}, s32[]{:S(2)}) async-start(s8[9437184]{0:T(1024)(128)(4,1)} %bitcast.4), calls=%async_computation.3 | async-start | bytes 2097152
  0.7 9.2 %collective-permute-start.4 = (f32[128,128]{1,0:T(8,128)}, f32[128,128]{1,0:T(8,128)S(1)}, u32[]{:S(2)}, u32[]{:S(2)}) collective-permute-start(f32[128,128]{1,0:T(8,128)} %bitcast.12), channel_id=1, source_target_pairs={{0,16},{16,0},{1,17},{17,1},{2,18},{18,2},{3,19},{19,3},{4,20},{20... | collective-permute-start | bytes 196616 | tf_op jit(solution)/shard_map/ppermute | solution.py:304
  1.2 1.1 %copy-start = (f32[1,1,1,128,128]{4,3,2,1,0:T(8,128)S(1)}, f32[1,1,1,128,128]{4,3,2,1,0:T(8,128)}, u32[]{:S(2)}) copy-start(f32[1,1,1,128,128]{4,3,2,1,0:T(8,128)} %param.2) | copy-start | bytes 196612
  2.4 9.4 %collective-permute-start.2 = (f32[64,128]{1,0:T(8,128)S(1)}, f32[64,128]{1,0:T(8,128)S(1)}, u32[]{:S(2)}, u32[]{:S(2)}) collective-permute-start(f32[64,128]{1,0:T(8,128)S(1)} %get-tuple-element.20), channel_id=1, source_target_pairs={{0,12},{4,8},{8,4},{12,0},{1,13},{5,9},{9,5},{13,1},{2,14},{6,10},... | collective-permute-start | bytes 98312 | tf_op jit(solution)/shard_map/ppermute | solution.py:304
  5.7 7.8 %collective-permute-start = (f32[64,128]{1,0:T(8,128)S(1)}, f32[64,128]{1,0:T(8,128)S(1)}, u32[]{:S(2)}, u32[]{:S(2)}) collective-permute-start(f32[64,128]{1,0:T(8,128)S(1)} %get-tuple-element.18), channel_id=1, source_target_pairs={{0,4},{4,0},{8,12},{12,8},{1,5},{5,1},{9,13},{13,9},{2,6},{6,2},{1... | collective-permute-start | bytes 98312 | tf_op jit(solution)/shard_map/ppermute | solution.py:304
  6.3 5.4 %collective-permute-start.3 = (f32[16,128]{1,0:T(8,128)S(1)}, f32[16,128]{1,0:T(8,128)S(1)}, u32[]{:S(2)}, u32[]{:S(2)}) collective-permute-start(f32[16,128]{1,0:T(8,128)S(1)} %get-tuple-element.21), channel_id=1, source_target_pairs={{0,3},{1,2},{2,1},{3,0},{4,7},{5,6},{6,5},{7,4},{8,11},{9,10},{10,... | collective-permute-start | bytes 24584 | tf_op jit(solution)/shard_map/ppermute | solution.py:304
  9.9 3.7 %collective-permute-start.1 = (f32[16,128]{1,0:T(8,128)S(1)}, f32[16,128]{1,0:T(8,128)S(1)}, u32[]{:S(2)}, u32[]{:S(2)}) collective-permute-start(f32[16,128]{1,0:T(8,128)S(1)} %get-tuple-element.19), channel_id=1, source_target_pairs={{0,1},{1,0},{2,3},{3,2},{4,5},{5,4},{6,7},{7,6},{8,9},{9,8},{10,11... | collective-permute-start | bytes 24584 | tf_op jit(solution)/shard_map/ppermute | solution.py:304
  14.4 4.7 %collective-permute-start.9 = (f32[128,128]{1,0:T(8,128)S(1)}, f32[128,128]{1,0:T(8,128)S(1)}, u32[]{:S(2)}, u32[]{:S(2)}) collective-permute-start(f32[128,128]{1,0:T(8,128)S(1)} %get-tuple-element.23.src.refs_0_), channel_id=1, source_target_pairs={{0,16},{16,0},{1,17},{17,1},{2,18},{18,2},{3,19},{19,3},{4,20},{20... | collective-permute-start | bytes 196616 | tf_op jit(solution)/shard_map/ppermute | solution.py:304
  14.5 7.5 %collective-permute-start.7 = (f32[64,128]{1,0:T(8,128)S(1)}, f32[64,128]{1,0:T(8,128)S(1)}, u32[]{:S(2)}, u32[]{:S(2)}) collective-permute-start(f32[64,128]{1,0:T(8,128)S(1)} %get-tuple-element.26), channel_id=1, source_target_pairs={{0,12},{4,8},{8,4},{12,0},{1,13},{5,9},{9,5},{13,1},{2,14},{6,10},... | collective-permute-start | bytes 98312 | tf_op jit(solution)/shard_map/ppermute | solution.py:304
  16.0 6.8 %collective-permute-start.5 = (f32[64,128]{1,0:T(8,128)S(1)}, f32[64,128]{1,0:T(8,128)S(1)}, u32[]{:S(2)}, u32[]{:S(2)}) collective-permute-start(f32[64,128]{1,0:T(8,128)S(1)} %get-tuple-element.24), channel_id=1, source_target_pairs={{0,4},{4,0},{8,12},{12,8},{1,5},{5,1},{9,13},{13,9},{2,6},{6,2},{1... | collective-permute-start | bytes 98312 | tf_op jit(solution)/shard_map/ppermute | solution.py:304
  16.5 5.4 %collective-permute-start.8 = (f32[16,128]{1,0:T(8,128)S(1)}, f32[16,128]{1,0:T(8,128)S(1)}, u32[]{:S(2)}, u32[]{:S(2)}) collective-permute-start(f32[16,128]{1,0:T(8,128)S(1)} %get-tuple-element.27), channel_id=1, source_target_pairs={{0,3},{1,2},{2,1},{3,0},{4,7},{5,6},{6,5},{7,4},{8,11},{9,10},{10,... | collective-permute-start | bytes 24584 | tf_op jit(solution)/shard_map/ppermute | solution.py:304
  19.1 3.7 %collective-permute-start.6 = (f32[16,128]{1,0:T(8,128)S(1)}, f32[16,128]{1,0:T(8,128)S(1)}, u32[]{:S(2)}, u32[]{:S(2)}) collective-permute-start(f32[16,128]{1,0:T(8,128)S(1)} %get-tuple-element.25), channel_id=1, source_target_pairs={{0,1},{1,0},{2,3},{3,2},{4,5},{5,4},{6,7},{7,6},{8,9},{9,8},{10,11... | collective-permute-start | bytes 24584 | tf_op jit(solution)/shard_map/ppermute | solution.py:304

commit v2 on v1

--- a/solution.py
+++ b/solution.py
@@ -21,20 +21,20 @@
 mass_shift = 4.0
 epsilon = 1e-06
 f32 = jnp.float32
-ORDER = ("tb", "x", "zb", "ta", "za")
+EDGES = (("tb", "zb", "ta", "za"), ("tb", "zb", "ta", "za"))
+ORDERS = (("tb", "x", "zb", "ta", "za"), ("tb", "x", "zb", "ta", "za"))
 FIRST_COST = 20_000_000_000
 
-VMEM_SPEC = pl.BlockSpec(memory_space=pltpu.VMEM)
 PARAMS = pltpu.CompilerParams(vmem_limit_bytes=12 * 1024 * 1024)
 
 
-def call(body, outs, scratch=(), cost=None):
+def call(body, outs, scratch=(), cost=None, space=pltpu.VMEM):
     if cost is not None:
         cost = pl.CostEstimate(flops=cost, bytes_accessed=0, transcendentals=0)
     return pl.pallas_call(
         body,
         out_shape=[jax.ShapeDtypeStruct(o, f32) for o in outs],
-        out_specs=[VMEM_SPEC] * len(outs),
+        out_specs=[pl.BlockSpec(memory_space=space)] * len(outs),
         scratch_shapes=list(scratch),
         compiler_params=PARAMS,
         cost_estimate=cost,
@@ -64,7 +64,7 @@
     write_faces(src_ref, *outs)
 
 
-def multiply(fields, links, groups, red, out, add=None):
+def multiply(fields, links, groups, red, out, add=None, unroll=False):
     def chunk(cb, carry):
         acc = [None] * (2 * RHS * SUB)
         for field, dirs in groups:
@@ -98,7 +98,7 @@
             out[where, :] = total
         return carry
 
-    lax.fori_loop(0, TILES, chunk, 0)
+    lax.fori_loop(0, TILES, chunk, 0, unroll=unroll)
 
 
 RED = pltpu.VMEM((2 * RHS * SUB * SUB, S), f32)
@@ -130,24 +130,38 @@
 PAD = pltpu.VMEM((3 * S, VEC), f32)
 
 
-def edge_fields(own, z_edge, t_edge, which, fields, at, pad):
-    dirs = []
-    for k, axis in enumerate(("gz", "ta")):
-        down = (lax.axis_index(axis) + which) % 2
-        if axis == "gz":
-            fields[at] = assemble_z(own, z_edge, down == 0)
-        else:
-            fields[at + 1] = assemble_t(own, t_edge, down == 0, pad)
-        dirs.append((at + k, (5 + 2 * k + down,)))
-    return tuple(dirs)
-
-
-def local_part(n_x, with_copy):
+def edge_part(edge, src, piece, links, part, out_t, fields, red, pad):
+    axis, which = ("gz" if edge[0] == "z" else "ta"), (1 if edge[1] == "b" else 0)
+    down = (lax.axis_index(axis) + which) % 2
+    if axis == "gz":
+        fields[0] = assemble_z(src[...], piece[...], down == 0)
+        first = 5
+    else:
+        fields[0] = assemble_t(src[...], piece[...], down == 0, pad)
+        first = 7
+    multiply(fields, links, ((0, (first + down,)),), red, out_t, part, True)
+
+
+EDGE_SCRATCH = (pltpu.VMEM((1, VEC, S), f32), RED, PAD)
+
+
+def add_edge(edge, *args):
+    body = lambda *refs: edge_part(edge, *refs)
+    return call(body, ((VEC, S),), EDGE_SCRATCH)(*args)[0]
+
+
+def rotated(v):
+    lane = lax.broadcasted_iota(jnp.int32, v.shape, 1)
+    real = (lane // DOF) % 2 == 0
+    return jnp.where(real, -pltpu.roll(v, VEC - DOF, 1), pltpu.roll(v, DOF, 1))
+
+
+def local_part(n_x, second):
     def body(src, *refs):
         xs = [x[...] for x in refs[:n_x]]
         if n_x == 2:
             xs = swap_halves("xy", *xs)
-        links, part = refs[n_x : n_x + 2]
+        links = refs[n_x]
         fields, red = refs[-2:]
         own = src[...]
         step = CZ * CT
@@ -156,37 +170,29 @@
         fields[2] = jnp.concatenate([own[S - step :], own[: S - step]], axis=0).T
         for i, x in enumerate(xs):
             fields[3 + i] = x.T
-        if with_copy:
-            refs[n_x + 2][...] = fields[0]
+        if second:
+            zero, part, rot_zero, rot_first = refs[n_x + 1 : n_x + 5]
+            rot_zero[...] = rotated(zero[...])
+            rot_first[...] = rotated(own)
+        else:
+            part, src_t = refs[n_x + 1 : n_x + 3]
+            src_t[...] = fields[0]
         dirs = ((0, (0,)), (1, (3,)), (2, (4,)))
         dirs += ((3, (1, 2)),) if n_x == 1 else ((3, (1,)), (4, (2,)))
         multiply(fields, links, dirs, red, part)
 
-    outs = ((VEC, S),) * (2 if with_copy else 1)
+    outs = ((VEC, S),) + (((S, VEC),) * 2 if second else ((VEC, S),))
     return call(body, outs, (pltpu.VMEM((3 + n_x, VEC, S), f32), RED))
 
 
-LAST_SCRATCH = (pltpu.VMEM((2, VEC, S), f32), RED, PAD)
-
-
-def edge_part(which, src, ze, te, links, part, out_t, fields, red, pad):
-    dirs = edge_fields(src[...], ze[...], te[...], which, fields, 0, pad)
-    multiply(fields, links, dirs, red, out_t, part)
-
-
-def edge_body(*refs):
-    edge_part(1, *refs)
-
-
-def add_edges(*args):
-    return call(edge_body, ((VEC, S),), LAST_SCRATCH)(*args)[0]
-
-
-def first_body(src, za, ta, links, part, out_t, out, *refs):
-    faces, scratch = refs[:4], refs[4:]
-    edge_part(0, src, za, ta, links, part, out_t, *scratch)
-    out[...] = out_t[...].T
-    write_faces(out, *faces)
+def first_body(edge):
+    def body(src, piece, links, part, out_t, out, *refs):
+        faces, scratch = refs[:4], refs[4:]
+        edge_part(edge, src, piece, links, part, out_t, *scratch)
+        out[...] = out_t[...].T
+        write_faces(out, *faces)
+
+    return body
 
 
 def halves(ref, r):
@@ -207,18 +213,27 @@
 
 
 TERMS = 9
-
-
-def second_body(src, za, ta, links, part, first_t, zero_t, out_t, sums, *refs):
+TABLE = pltpu.VMEM((-(-TERMS * RHS // SUB) * SUB, S), f32)
+
+
+def slots(shape):
+    row = lax.broadcasted_iota(jnp.int32, shape, 0)
+    lane = lax.broadcasted_iota(jnp.int32, shape, 1)
+    r = sum((row >= TERMS * k).astype(jnp.int32) for k in range(1, RHS))
+    return (lane == (row - r * TERMS) * SUB + r) & (row < RHS * TERMS)
+
+
+def second_body(edge, src, piece, links, part, first_t, zero_t, out_t, sums, *refs):
     table, scratch = refs[-1], refs[:-1]
-    edge_part(0, src, za, ta, links, part, out_t, *scratch)
+    edge_part(edge, src, piece, links, part, out_t, *scratch)
     table[...] = jnp.zeros_like(table)
     for r in range(RHS):
         b, u, w = halves(zero_t, r), halves(first_t, r), halves(out_t, r)
         rows = square(b) + inner(b, u) + square(u) + inner(b, w) + inner(u, w) + square(w)
         for i, row in enumerate(rows):
             table[r * TERMS + i : r * TERMS + i + 1, :] = row
-    total = column(table[...].T)
+    total = jnp.sum(table[...], axis=1, keepdims=True)
+    total = column(jnp.where(slots(table.shape), total, 0.0))
     sums[...] = jnp.broadcast_to(total[None], sums.shape)
 
 
@@ -279,22 +294,51 @@
     return minus(y, times(t, q)), t
 
 
-def final_body(sums, zero_t, first_t, second_t, sol, res, stage):
-    total = jnp.sum(sums[...], axis=0)
-    stage[...] = jnp.broadcast_to(total, stage.shape).T
-    sol_rows = []
-    res_rows = []
+def per_lane(rows):
+    lane = lax.broadcasted_iota(jnp.int32, (1, VEC), 1)
+    out = rows[0:1, :]
+    for r in range(1, RHS):
+        out = jnp.where(lane < 2 * r * DOF, out, rows[r : r + 1, :])
+    return out
+
+
+def final_body(sums, zero, rot_zero, zero_t, first, rot_first, first_t, second_t, *refs):
+    sol, res, sol_stage, res_stage, sems = refs
+    total = jnp.broadcast_to(jnp.sum(sums[...], axis=0), (SUB, S))
+    row = lax.broadcasted_iota(jnp.int32, (SUB, S), 0)
+    lane = lax.broadcasted_iota(jnp.int32, (SUB, S), 1)
+    v = []
+    for i in range(TERMS):
+        value = jnp.sum(jnp.where(lane == i * SUB + row, total, 0.0), axis=1, keepdims=True)
+        v.append(jnp.broadcast_to(value, (SUB, S)))
+    a, t = coefficients(v[0], (v[1], v[2]), v[3], (v[4], v[5]), (v[6], v[7]), v[8])
+    sol_stage[...] = (
+        per_lane(a[0]) * zero[...]
+        + per_lane(a[1]) * rot_zero[...]
+        + per_lane(t[0]) * first[...]
+        + per_lane(t[1]) * rot_first[...]
+    )
+    sol_copy = pltpu.make_async_copy(sol_stage, sol, sems.at[0])
+    sol_copy.start()
+    keep = (1.0 - mass_shift * a[0], -mass_shift * a[1])
+    mixed = plus(scaled(mass_shift, t), a)
+    rows = []
     for r in range(RHS):
-        v = [stage[r * TERMS + i : r * TERMS + i + 1, :] for i in range(TERMS)]
-        a, t = coefficients(v[0], (v[1], v[2]), v[3], (v[4], v[5]), (v[6], v[7]), v[8])
+        at = lambda u: (u[0][r : r + 1, :], u[1][r : r + 1, :])
         b, u, w = halves(zero_t, r), halves(first_t, r), halves(second_t, r)
-        x = plus(times(a, b), times(t, u))
-        image = plus(scaled(mass_shift, x), plus(times(a, u), times(t, w)))
-        left = minus(b, image)
-        sol_rows += list(x)
-        res_rows += list(left)
-    sol[...] = jnp.concatenate(sol_rows, axis=0).T
-    res[...] = jnp.concatenate(res_rows, axis=0).T
+        rows += list(minus(minus(times(at(keep), b), times(at(mixed), u)), times(at(t), w)))
+    res_stage[...] = jnp.concatenate(rows, axis=0).T
+    res_copy = pltpu.make_async_copy(res_stage, res, sems.at[1])
+    res_copy.start()
+    sol_copy.wait()
+    res_copy.wait()
+
+
+FINAL_SCRATCH = (
+    pltpu.VMEM((S, VEC), f32),
+    pltpu.VMEM((S, VEC), f32),
+    pltpu.SemaphoreType.DMA((2,)),
+)
 
 
 def exchange(value, axis, offset):
@@ -306,7 +350,7 @@
     )
 
 
-def halo(value, faces):
+def halo(value, faces, order):
     za, zb, ta, tb = faces
     sent = {}
     plan = {
@@ -318,11 +362,10 @@
     }
     if lax.axis_size("xy") > 2:
         plan["x"].append(("xb", value, "xy", 1))
-    plan = [entry for key in ORDER for entry in plan[key]]
+    plan = [entry for key in order for entry in plan[key]]
     for key, piece, axis, offset in plan:
         sent[key] = exchange(piece, axis, offset)
-    xs = [sent[k] for k in ("xa", "xb") if k in sent]
-    return xs, [sent["zb"], sent["tb"]], [sent["za"], sent["ta"]]
+    return [sent[k] for k in ("xa", "xb") if k in sent], sent
 
 
 def shards(right_side, link_blocks):
@@ -333,23 +376,25 @@
     devices = lax.axis_size("xy") * lax.axis_size("gz") * lax.axis_size("ta")
 
     faces = call(faces_body, FACES, (), FIRST_COST)(b)
-    xs, early, late = halo(b, faces)
-    part, b_t = local_part(n_x, True)(b, *xs, links)
-    part = add_edges(b, *early, links, part)
+    xs, sent = halo(b, faces, ORDERS[0])
+    part, b_t = local_part(n_x, False)(b, *xs, links)
+    for edge in EDGES[0][:-1]:
+        part = add_edge(edge, b, sent[edge], links, part)
+    edge = EDGES[0][-1]
     u_t, u, *faces = call(
-        first_body, ((VEC, S), (S, VEC)) + FACES, LAST_SCRATCH
-    )(b, *late, links, part)
-    xs, early, late = halo(u, faces)
-    (part,) = local_part(n_x, False)(u, *xs, links)
-    part = add_edges(u, *early, links, part)
+        first_body(edge), ((VEC, S), (S, VEC)) + FACES, EDGE_SCRATCH
+    )(b, sent[edge], links, part)
+    xs, sent = halo(u, faces, ORDERS[1])
+    part, b_rot, u_rot = local_part(n_x, True)(u, *xs, links, b)
+    for edge in EDGES[1][:-1]:
+        part = add_edge(edge, u, sent[edge], links, part)
+    edge = EDGES[1][-1]
     w_t, sums = call(
-        second_body,
-        ((VEC, S), (devices, 1, S)),
-        LAST_SCRATCH + (pltpu.VMEM((S, S), f32),),
-    )(u, *late, links, part, u_t, b_t)
+        lambda *refs: second_body(edge, *refs), ((VEC, S), (devices, 1, S)), EDGE_SCRATCH + (TABLE,)
+    )(u, sent[edge], links, part, u_t, b_t)
     sums = lax.all_to_all(sums, AXES, 0, 0)
-    sol, res = call(final_body, ((S, VEC), (S, VEC)), (pltpu.VMEM((S, S), f32),))(
-        sums, b_t, u_t, w_t
+    sol, res = call(final_body, ((S, VEC),) * 2, FINAL_SCRATCH, None, pl.ANY)(
+        sums, b, b_rot, b_t, u, u_rot, u_t, w_t
     )
     return sol.reshape(right_side.shape), res.reshape(right_side.shape)
 

time: 36.6 us -> 37 us (1.011)
  Pallas kernels: 7 us -> 7.42 us
    pallas_call x7 -> x11, Pallas kernels: 6.98 us -> 7.41 us  [the longest x6 2.6 us: add_edge(): return call(body, ((VEC, S),), EDGE_SCRATCH)(*args)[0]]
  transfers between devices with their start and end apart: 10 -> 10, of which waited for: 3 -> 3; matrix products, arithmetic and copies ran while one was open for 0% -> 0% of each run, Pallas kernels for 12% -> 15%
where the time goes in v2:
time: 37 us; the launch traced here: 36.8 us
  starting transfers between devices  12.9 us (35%)
  blocking collectives  11.9 us (32%)
  Pallas kernels  7.42 us (20%)
  waiting for transfers between devices  2.67 us (7%)
  local copies, waits for them, and re-layouts  1.14 us (3%)
  between operations  0.79 us (2%)
    ppermute x10, starting transfers between devices, exchange(): lax.ppermute(value, axis, [(i, (i + 1 if (i - offset) % 2 == 0 else i - 1...  12.9 us
    all_to_all x1, blocking collectives, shards(): sums = lax.all_to_all(sums, AXES, 0, 0)  11.9 us
    ppermute x10, waiting for transfers between devices, exchange(): lax.ppermute(value, axis, [(i, (i + 1 if (i - offset) % 2 == 0 else i - 1...  2.67 us
    pallas_call x6, Pallas kernels, add_edge(): return call(body, ((VEC, S),), EDGE_SCRATCH)(*args)[0]  2.6 us
    pallas_call x1, Pallas kernels, shards(): part, b_rot, u_rot = local_part(n_x, True)(u, *xs, links, b)  1.44 us
    pallas_call x1, Pallas kernels, shards(): part, b_t = local_part(n_x, False)(b, *xs, links)  1.36 us
    unnamed x8, local copies, waits for them, and re-layouts  1.14 us
    pallas_call x1, Pallas kernels, shards(): call(final_body, ((S, VEC),) * 2, FINAL_SCRATCH, None, pl.ANY)  0.91 us
  transfers between devices with their start and end apart: 10, of which 3 were waited for; matrix products, arithmetic and copies ran while one was open for 0% of the time, Pallas kernels for 15%

profile of v2, /device:TPU:0, one launch (start us, length us, event | category | flops | bytes accessed | tf_op | source)
XLA Modules:
  0.0 36.8 jit_solution(3579906725431449682)
XLA Ops:
  0.6 0.0 slice-start
  0.6 0.0 slice-start.1
  0.7 0.0 slice-start.2
  0.7 0.6 %collective-permute-start.4 = (f32[128,128]{1,0:T(8,128)}, f32[128,128]{1,0:T(8,128)S(1)}, u32[]{:S(2)}, u32[]{:S(2)}) collective-permute-start(f32[128,128]{1,0:T(8,128)} %bitcast.16), channel_id=1, source_target_pairs={{0,16},{16,0},{1,17},{17,1},{2,18},{18,2},{3,19},{19,3},{4,20},{20... | collective-permute-start | bytes 196616 | tf_op jit(solution)/shard_map/ppermute | solution.py:348
  1.2 0.0 copy-start
  1.2 1.1 %copy-done = f32[1,1,1,128,128]{4,3,2,1,0:T(8,128)S(1)} copy-done((f32[1,1,1,128,128]{4,3,2,1,0:T(8,128)S(1)}, f32[1,1,1,128,128]{4,3,2,1,0:T(8,128)}, u32[]{:S(2)}) %copy-start) | copy-done | bytes 65560
  2.4 3.4 %collective-permute-start.2 = (f32[64,128]{1,0:T(8,128)S(1)}, f32[64,128]{1,0:T(8,128)S(1)}, u32[]{:S(2)}, u32[]{:S(2)}) collective-permute-start(f32[64,128]{1,0:T(8,128)S(1)} %get-tuple-element.23), channel_id=1, source_target_pairs={{0,12},{4,8},{8,4},{12,0},{1,13},{5,9},{9,5},{13,1},{2,14},{6,10},... | collective-permute-start | bytes 98312 | tf_op jit(solution)/shard_map/ppermute | solution.py:348
  5.7 0.5 %collective-permute-start = (f32[64,128]{1,0:T(8,128)S(1)}, f32[64,128]{1,0:T(8,128)S(1)}, u32[]{:S(2)}, u32[]{:S(2)}) collective-permute-start(f32[64,128]{1,0:T(8,128)S(1)} %get-tuple-element.21), channel_id=1, source_target_pairs={{0,4},{4,0},{8,12},{12,8},{1,5},{5,1},{9,13},{13,9},{2,6},{6,2},{1... | collective-permute-start | bytes 98312 | tf_op jit(solution)/shard_map/ppermute | solution.py:348
  6.3 3.6 %collective-permute-start.3 = (f32[16,128]{1,0:T(8,128)S(1)}, f32[16,128]{1,0:T(8,128)S(1)}, u32[]{:S(2)}, u32[]{:S(2)}) collective-permute-start(f32[16,128]{1,0:T(8,128)S(1)} %get-tuple-element.24), channel_id=1, source_target_pairs={{0,3},{1,2},{2,1},{3,0},{4,7},{5,6},{6,5},{7,4},{8,11},{9,10},{10,... | collective-permute-start | bytes 24584 | tf_op jit(solution)/shard_map/ppermute | solution.py:348
  9.9 0.0 collective-permute-start.1
  9.9 0.0 collective-permute-done.4.refs_0_
  9.9 0.0 slice-done
  9.9 0.0 slice-done.1
  9.9 0.0 slice-done.2
  9.9 1.4 %shard_map.42 = (f32[128,128]{1,0:T(8,128)S(1)}, f32[128,128]{1,0:T(8,128)S(1)}) custom-call(f32[128,128]{1,0:T(8,128)S(1)} %bitcast.18, f32[128,128]{1,0:T(8,128)S(1)} %collective-permute-done.4.refs_0_, f32[9,2,32,32,128]{4,3,2,1,0:T(8,128)S(1)} %bitcast.6), custom_call_target="tpu_custom_call" | custom-call | tf_op jit(solution)/shard_map/pallas_call | solution.py:380
  11.3 0.4 %collective-permute-done.3.refs_1_ = f32[16,128]{1,0:T(8,128)S(1)} collective-permute-done((f32[16,128]{1,0:T(8,128)S(1)}, f32[16,128]{1,0:T(8,128)S(1)}, u32[]{:S(2)}, u32[]{:S(2)}) %collective-permute-start.3) | collective-permute-done | bytes 8224 | tf_op jit(solution)/shard_map/ppermute | solution.py:348
  11.7 0.4 %shard_map.43.refs_3_ = f32[128,128]{1,0:T(8,128)S(1)} custom-call(f32[128,128]{1,0:T(8,128)S(1)} %bitcast.19, f32[16,128]{1,0:T(8,128)S(1)} %collective-permute-done.3.refs_1_, f32[9,2,32,32,128]{4,3,2,1,0:T(8,128)S(1)} %bitcast.7, f32[128,128]{1,0:T(8,128)S(1)} %get-tuple-element.25.refs_3_), custom_call_target="tpu_custom_call" | custom-call | tf_op jit(solution)/shard_map/pallas_call | solution.py:150
  12.2 0.0 collective-permute-done.2.refs_1_
  12.2 0.4 %shard_map.44.refs_3_ = f32[128,128]{1,0:T(8,128)S(1)} custom-call(f32[128,128]{1,0:T(8,128)S(1)} %bitcast.20, f32[64,128]{1,0:T(8,128)S(1)} %collective-permute-done.2.refs_1_, f32[9,2,32,32,128]{4,3,2,1,0:T(8,128)S(1)} %bitcast.8, f32[128,128]{1,0:T(8,128)S(1)} %shard_map.43.refs_3_), custom_call_target="tpu_custom_call" | custom-call | tf_op jit(solution)/shard_map/pallas_call | solution.py:150
  12.6 0.9 %collective-permute-done.1.refs_1_ = f32[16,128]{1,0:T(8,128)S(1)} collective-permute-done((f32[16,128]{1,0:T(8,128)S(1)}, f32[16,128]{1,0:T(8,128)S(1)}, u32[]{:S(2)}, u32[]{:S(2)}) %collective-permute-start.1) | collective-permute-done | bytes 8224 | tf_op jit(solution)/shard_map/ppermute | solution.py:348
  13.5 0.4 %shard_map.45.part = f32[128,128]{1,0:T(8,128)S(1)} custom-call(f32[128,128]{1,0:T(8,128)S(1)} %bitcast.21, f32[16,128]{1,0:T(8,128)S(1)} %collective-permute-done.1.refs_1_, f32[9,2,32,32,128]{4,3,2,1,0:T(8,128)S(1)} %bitcast.9, f32[128,128]{1,0:T(8,128)S(1)} %shard_map.44.refs_3_), custom_call_target="tpu_custom_call" | custom-call | tf_op jit(solution)/shard_map/pallas_call | solution.py:150
  14.0 0.0 collective-permute-done.piece
  14.0 0.5 %shard_map.46 = (f32[128,128]{1,0:T(8,128)S(1)}, f32[128,128]{1,0:T(8,128)S(1)}, f32[64,128]{1,0:T(8,128)S(1)}, f32[64,128]{1,0:T(8,128)S(1)}, f32[16,128]{1,0:T(8,128)S(1)}, /*index=5*/f32[16,128]{1,0:T(8,128)S(1)}) custom-call(f32[128,128]{1,0:T(8,128)S(1)} %bitcast.22, f32[64,128]{1,0:T(8,128)S(1)} %collective-permute-done.piece, ...), custom_call_target="tpu_custom_call" | custom-call | tf_op jit(solution)/shard_map/pallas_call | solution.py:384
  14.5 0.1 collective-permute-start.9
  14.6 1.5 %collective-permute-start.7 = (f32[64,128]{1,0:T(8,128)S(1)}, f32[64,128]{1,0:T(8,128)S(1)}, u32[]{:S(2)}, u32[]{:S(2)}) collective-permute-start(f32[64,128]{1,0:T(8,128)S(1)} %get-tuple-element.29), channel_id=1, source_target_pairs={{0,12},{4,8},{8,4},{12,0},{1,13},{5,9},{9,5},{13,1},{2,14},{6,10},... | collective-permute-start | bytes 98312 | tf_op jit(solution)/shard_map/ppermute | solution.py:348
  16.1 0.5 %collective-permute-start.5 = (f32[64,128]{1,0:T(8,128)S(1)}, f32[64,128]{1,0:T(8,128)S(1)}, u32[]{:S(2)}, u32[]{:S(2)}) collective-permute-start(f32[64,128]{1,0:T(8,128)S(1)} %get-tuple-element.27), channel_id=1, source_target_pairs={{0,4},{4,0},{8,12},{12,8},{1,5},{5,1},{9,13},{13,9},{2,6},{6,2},{1... | collective-permute-start | bytes 98312 | tf_op jit(solution)/shard_map/ppermute | solution.py:348
  16.6 2.7 %collective-permute-start.8 = (f32[16,128]{1,0:T(8,128)S(1)}, f32[16,128]{1,0:T(8,128)S(1)}, u32[]{:S(2)}, u32[]{:S(2)}) collective-permute-start(f32[16,128]{1,0:T(8,128)S(1)} %get-tuple-element.30), channel_id=1, source_target_pairs={{0,3},{1,2},{2,1},{3,0},{4,7},{5,6},{6,5},{7,4},{8,11},{9,10},{10,... | collective-permute-start | bytes 24584 | tf_op jit(solution)/shard_map/ppermute | solution.py:348
  19.3 0.0 collective-permute-start.6
  19.3 0.0 collective-permute-done.9.refs_0_
  19.3 1.4 %shard_map.47 = (f32[128,128]{1,0:T(8,128)S(1)}, f32[128,128]{1,0:T(8,128)S(1)}, f32[128,128]{1,0:T(8,128)S(1)}) custom-call(f32[128,128]{1,0:T(8,128)S(1)} %get-tuple-element.26.src.refs_0_.first, f32[128,128]{1,0:T(8,128)S(1)} %collective-permute-done.9.refs_0_, f32[9,2,32,32,128]{4,3,2,1,0:T(8,128)S(1)} %bitcast.11, f32[128,128]{1,0:T(8,128)S(1)} %bitcast.23), custom_call_target="tpu_custom_call" | custom-call | tf_op jit(solution)/shard_map/pallas_call | solution.py:388
  20.8 1.3 %collective-permute-done.8.refs_1_ = f32[16,128]{1,0:T(8,128)S(1)} collective-permute-done((f32[16,128]{1,0:T(8,128)S(1)}, f32[16,128]{1,0:T(8,128)S(1)}, u32[]{:S(2)}, u32[]{:S(2)}) %collective-permute-start.8) | collective-permute-done | bytes 8224 | tf_op jit(solution)/shard_map/ppermute | solution.py:348
  22.1 0.4 %shard_map.48.refs_3_ = f32[128,128]{1,0:T(8,128)S(1)} custom-call(f32[128,128]{1,0:T(8,128)S(1)} %get-tuple-element.26.src.refs_0_.first, f32[16,128]{1,0:T(8,128)S(1)} %collective-permute-done.8.refs_1_, f32[9,2,32,32,128]{4,3,2,1,0:T(8,128)S(1)} %bitcast.12, f32[128,128]{1,0:T(8,128)S(1)} %get-tuple-element.31.refs_3_), custom_call_target="tpu_custom_call" | custom-call | tf_op jit(solution)/shard_map/pallas_call | solution.py:150
  22.5 0.0 collective-permute-done.7.refs_1_
  22.5 0.4 %shard_map.49.refs_3_ = f32[128,128]{1,0:T(8,128)S(1)} custom-call(f32[128,128]{1,0:T(8,128)S(1)} %get-tuple-element.26.src.refs_0_.first, f32[64,128]{1,0:T(8,128)S(1)} %collective-permute-done.7.refs_1_, f32[9,2,32,32,128]{4,3,2,1,0:T(8,128)S(1)} %bitcast.13, f32[128,128]{1,0:T(8,128)S(1)} %shard_map.48.refs_3_), custom_call_target="tpu_custom_call" | custom-call | tf_op jit(solution)/shard_map/pallas_call | solution.py:150
  22.9 0.0 collective-permute-done.6.refs_1_
  23.0 0.4 %shard_map.50.refs_3_ = f32[128,128]{1,0:T(8,128)S(1)} custom-call(f32[128,128]{1,0:T(8,128)S(1)} %get-tuple-element.26.src.refs_0_.first, f32[16,128]{1,0:T(8,128)S(1)} %collective-permute-done.6.refs_1_, f32[9,2,32,32,128]{4,3,2,1,0:T(8,128)S(1)} %bitcast.14, f32[128,128]{1,0:T(8,128)S(1)} %shard_map.49.refs_3_), custom_call_target="tpu_custom_call" | custom-call | tf_op jit(solution)/shard_map/pallas_call | solution.py:150
  23.4 0.0 collective-permute-done.5.refs_1_
  23.4 0.6 %shard_map.51 = (f32[128,128]{1,0:T(8,128)S(1)}, f32[32,1,128]{2,1,0:T(1,128)S(1)}) custom-call(f32[128,128]{1,0:T(8,128)S(1)} %get-tuple-element.26.src.refs_0_.first, f32[64,128]{1,0:T(8,128)S(1)} %collective-permute-done.5.refs_1_, f32[9,2,32,32,128]{4,3,2,1,0:T(8,128)S(1)} %bitcast.15, f32[128,128]{1,0:T(8,128)S(1)} %shard_map.50.refs_3_, ...), custom_call_target="tpu_custom_call" | custom-call | tf_op jit(solution)/shard_map/pallas_call | solution.py:392
  24.0 11.9 %all_to_all.5.sums = f32[32,1,128]{2,1,0:T(1,128)S(1)} all-to-all(f32[32,1,128]{2,1,0:T(1,128)S(1)} %get-tuple-element.34), channel_id=1, replica_groups=mesh['xy'=2,'gz'=4,'ta'=4] {'xy','gz','ta'}, dimensions={0} | all-to-all | bytes 32768 | tf_op jit(solution)/shard_map/all_to_all | solution.py:395
  35.9 0.9 %shard_map.52 = (f32[128,128]{1,0:T(8,128)}, f32[128,128]{1,0:T(8,128)}) custom-call(f32[32,1,128]{2,1,0:T(1,128)S(1)} %all_to_all.5.sums, f32[128,128]{1,0:T(8,128)S(1)} %bitcast.24, f32[128,128]{1,0:T(8,128)S(1)} %get-tuple-element.35.rot_zero, f32[128,128]{1,0:T(8,128)S(1)} %get-tuple-element.33.refs_5_.zero_t, ...), custom_call_target="tpu_custom_call" | custom-call | tf_op jit(solution)/shard_map/pallas_call | solution.py:396
  (2 shorter events, 0.0 us)
Async XLA Ops:
  0.6 9.3 %slice-start = ((s8[9437184]{0:T(1024)(128)(4,1)}), s8[4194304]{0:T(1024)(128)(4,1)S(1)}, s32[]{:S(2)}) async-start(s8[9437184]{0:T(1024)(128)(4,1)} %bitcast.4), calls=%async_computation.1 | async-start | bytes 8388608
  0.6 9.2 %slice-start.1 = ((s8[9437184]{0:T(1024)(128)(4,1)}), s8[4194304]{0:T(1024)(128)(4,1)S(1)}, s32[]{:S(2)}) async-start(s8[9437184]{0:T(1024)(128)(4,1)} %bitcast.4), calls=%async_computation.2 | async-start | bytes 8388608
  0.7 9.2 %slice-start.2 = ((s8[9437184]{0:T(1024)(128)(4,1)}), s8[1048576]{0:T(1024)(128)(4,1)S(1)}, s32[]{:S(2)}) async-start(s8[9437184]{0:T(1024)(128)(4,1)} %bitcast.4), calls=%async_computation.3 | async-start | bytes 2097152
  0.7 9.2 %collective-permute-start.4 = (f32[128,128]{1,0:T(8,128)}, f32[128,128]{1,0:T(8,128)S(1)}, u32[]{:S(2)}, u32[]{:S(2)}) collective-permute-start(f32[128,128]{1,0:T(8,128)} %bitcast.16), channel_id=1, source_target_pairs={{0,16},{16,0},{1,17},{17,1},{2,18},{18,2},{3,19},{19,3},{4,20},{20... | collective-permute-start | bytes 196616 | tf_op jit(solution)/shard_map/ppermute | solution.py:348
  1.2 1.1 %copy-start = (f32[1,1,1,128,128]{4,3,2,1,0:T(8,128)S(1)}, f32[1,1,1,128,128]{4,3,2,1,0:T(8,128)}, u32[]{:S(2)}) copy-start(f32[1,1,1,128,128]{4,3,2,1,0:T(8,128)} %param.2) | copy-start | bytes 196612
  2.4 9.8 %collective-permute-start.2 = (f32[64,128]{1,0:T(8,128)S(1)}, f32[64,128]{1,0:T(8,128)S(1)}, u32[]{:S(2)}, u32[]{:S(2)}) collective-permute-start(f32[64,128]{1,0:T(8,128)S(1)} %get-tuple-element.23), channel_id=1, source_target_pairs={{0,12},{4,8},{8,4},{12,0},{1,13},{5,9},{9,5},{13,1},{2,14},{6,10},... | collective-permute-start | bytes 98312 | tf_op jit(solution)/shard_map/ppermute | solution.py:348
  5.7 8.2 %collective-permute-start = (f32[64,128]{1,0:T(8,128)S(1)}, f32[64,128]{1,0:T(8,128)S(1)}, u32[]{:S(2)}, u32[]{:S(2)}) collective-permute-start(f32[64,128]{1,0:T(8,128)S(1)} %get-tuple-element.21), channel_id=1, source_target_pairs={{0,4},{4,0},{8,12},{12,8},{1,5},{5,1},{9,13},{13,9},{2,6},{6,2},{1... | collective-permute-start | bytes 98312 | tf_op jit(solution)/shard_map/ppermute | solution.py:348
  6.3 5.4 %collective-permute-start.3 = (f32[16,128]{1,0:T(8,128)S(1)}, f32[16,128]{1,0:T(8,128)S(1)}, u32[]{:S(2)}, u32[]{:S(2)}) collective-permute-start(f32[16,128]{1,0:T(8,128)S(1)} %get-tuple-element.24), channel_id=1, source_target_pairs={{0,3},{1,2},{2,1},{3,0},{4,7},{5,6},{6,5},{7,4},{8,11},{9,10},{10,... | collective-permute-start | bytes 24584 | tf_op jit(solution)/shard_map/ppermute | solution.py:348
  9.9 3.7 %collective-permute-start.1 = (f32[16,128]{1,0:T(8,128)S(1)}, f32[16,128]{1,0:T(8,128)S(1)}, u32[]{:S(2)}, u32[]{:S(2)}) collective-permute-start(f32[16,128]{1,0:T(8,128)S(1)} %get-tuple-element.22), channel_id=1, source_target_pairs={{0,1},{1,0},{2,3},{3,2},{4,5},{5,4},{6,7},{7,6},{8,9},{9,8},{10,11... | collective-permute-start | bytes 24584 | tf_op jit(solution)/shard_map/ppermute | solution.py:348
  14.5 4.8 %collective-permute-start.9 = (f32[128,128]{1,0:T(8,128)S(1)}, f32[128,128]{1,0:T(8,128)S(1)}, u32[]{:S(2)}, u32[]{:S(2)}) collective-permute-start(f32[128,128]{1,0:T(8,128)S(1)} %get-tuple-element.26.src.refs_0_.first), channel_id=1, source_target_pairs={{0,16},{16,0},{1,17},{17,1},{2,18},{18,2},{3,19},{19,3},{4,20},{20... | collective-permute-start | bytes 196616 | tf_op jit(solution)/shard_map/ppermute | solution.py:348
  14.6 7.9 %collective-permute-start.7 = (f32[64,128]{1,0:T(8,128)S(1)}, f32[64,128]{1,0:T(8,128)S(1)}, u32[]{:S(2)}, u32[]{:S(2)}) collective-permute-start(f32[64,128]{1,0:T(8,128)S(1)} %get-tuple-element.29), channel_id=1, source_target_pairs={{0,12},{4,8},{8,4},{12,0},{1,13},{5,9},{9,5},{13,1},{2,14},{6,10},... | collective-permute-start | bytes 98312 | tf_op jit(solution)/shard_map/ppermute | solution.py:348
  16.1 7.3 %collective-permute-start.5 = (f32[64,128]{1,0:T(8,128)S(1)}, f32[64,128]{1,0:T(8,128)S(1)}, u32[]{:S(2)}, u32[]{:S(2)}) collective-permute-start(f32[64,128]{1,0:T(8,128)S(1)} %get-tuple-element.27), channel_id=1, source_target_pairs={{0,4},{4,0},{8,12},{12,8},{1,5},{5,1},{9,13},{13,9},{2,6},{6,2},{1... | collective-permute-start | bytes 98312 | tf_op jit(solution)/shard_map/ppermute | solution.py:348
  16.6 5.4 %collective-permute-start.8 = (f32[16,128]{1,0:T(8,128)S(1)}, f32[16,128]{1,0:T(8,128)S(1)}, u32[]{:S(2)}, u32[]{:S(2)}) collective-permute-start(f32[16,128]{1,0:T(8,128)S(1)} %get-tuple-element.30), channel_id=1, source_target_pairs={{0,3},{1,2},{2,1},{3,0},{4,7},{5,6},{6,5},{7,4},{8,11},{9,10},{10,... | collective-permute-start | bytes 24584 | tf_op jit(solution)/shard_map/ppermute | solution.py:348
  19.3 3.7 %collective-permute-start.6 = (f32[16,128]{1,0:T(8,128)S(1)}, f32[16,128]{1,0:T(8,128)S(1)}, u32[]{:S(2)}, u32[]{:S(2)}) collective-permute-start(f32[16,128]{1,0:T(8,128)S(1)} %get-tuple-element.28), channel_id=1, source_target_pairs={{0,1},{1,0},{2,3},{3,2},{4,5},{5,4},{6,7},{7,6},{8,9},{9,8},{10,11... | collective-permute-start | bytes 24584 | tf_op jit(solution)/shard_map/ppermute | solution.py:348

commit v3 on v2

--- a/solution.py
+++ b/solution.py
@@ -21,8 +21,9 @@
 mass_shift = 4.0
 epsilon = 1e-06
 f32 = jnp.float32
-EDGES = (("tb", "zb", "ta", "za"), ("tb", "zb", "ta", "za"))
-ORDERS = (("tb", "x", "zb", "ta", "za"), ("tb", "x", "zb", "ta", "za"))
+LOCAL_UNROLL = True
+EDGES = (("tb", "zb", "ta", "za"), ("zb", "za", "tb", "ta"))
+ORDERS = (("tb", "x", "zb", "ta", "za"), ("zb", "x", "za", "tb", "ta"))
 FIRST_COST = 20_000_000_000
 
 PARAMS = pltpu.CompilerParams(vmem_limit_bytes=12 * 1024 * 1024)
@@ -150,38 +151,28 @@
     return call(body, ((VEC, S),), EDGE_SCRATCH)(*args)[0]
 
 
-def rotated(v):
-    lane = lax.broadcasted_iota(jnp.int32, v.shape, 1)
-    real = (lane // DOF) % 2 == 0
-    return jnp.where(real, -pltpu.roll(v, VEC - DOF, 1), pltpu.roll(v, DOF, 1))
-
-
 def local_part(n_x, second):
     def body(src, *refs):
         xs = [x[...] for x in refs[:n_x]]
         if n_x == 2:
             xs = swap_halves("xy", *xs)
-        links = refs[n_x]
+        links, part = refs[n_x : n_x + 2]
         fields, red = refs[-2:]
-        own = src[...]
+        if second:
+            fields[0] = src[...]
+        else:
+            fields[0] = src[...].T
+            refs[n_x + 2][...] = fields[0]
         step = CZ * CT
-        fields[0] = own.T
-        fields[1] = jnp.concatenate([own[step:], own[:step]], axis=0).T
-        fields[2] = jnp.concatenate([own[S - step :], own[: S - step]], axis=0).T
+        fields[1] = pltpu.roll(fields[0], S - step, 1)
+        fields[2] = pltpu.roll(fields[0], step, 1)
         for i, x in enumerate(xs):
             fields[3 + i] = x.T
-        if second:
-            zero, part, rot_zero, rot_first = refs[n_x + 1 : n_x + 5]
-            rot_zero[...] = rotated(zero[...])
-            rot_first[...] = rotated(own)
-        else:
-            part, src_t = refs[n_x + 1 : n_x + 3]
-            src_t[...] = fields[0]
         dirs = ((0, (0,)), (1, (3,)), (2, (4,)))
         dirs += ((3, (1, 2)),) if n_x == 1 else ((3, (1,)), (4, (2,)))
-        multiply(fields, links, dirs, red, part)
-
-    outs = ((VEC, S),) + (((S, VEC),) * 2 if second else ((VEC, S),))
+        multiply(fields, links, dirs, red, part, None, LOCAL_UNROLL)
+
+    outs = ((VEC, S),) * (1 if second else 2)
     return call(body, outs, (pltpu.VMEM((3 + n_x, VEC, S), f32), RED))
 
 
@@ -223,7 +214,7 @@
     return (lane == (row - r * TERMS) * SUB + r) & (row < RHS * TERMS)
 
 
-def second_body(edge, src, piece, links, part, first_t, zero_t, out_t, sums, *refs):
+def second_body(edge, src, first_t, piece, links, part, zero_t, out_t, sums, *refs):
     table, scratch = refs[-1], refs[:-1]
     edge_part(edge, src, piece, links, part, out_t, *scratch)
     table[...] = jnp.zeros_like(table)
@@ -294,16 +285,7 @@
     return minus(y, times(t, q)), t
 
 
-def per_lane(rows):
-    lane = lax.broadcasted_iota(jnp.int32, (1, VEC), 1)
-    out = rows[0:1, :]
-    for r in range(1, RHS):
-        out = jnp.where(lane < 2 * r * DOF, out, rows[r : r + 1, :])
-    return out
-
-
-def final_body(sums, zero, rot_zero, zero_t, first, rot_first, first_t, second_t, *refs):
-    sol, res, sol_stage, res_stage, sems = refs
+def final_body(sums, zero_t, first_t, second_t, sol, res, sol_stage, res_stage, sems):
     total = jnp.broadcast_to(jnp.sum(sums[...], axis=0), (SUB, S))
     row = lax.broadcasted_iota(jnp.int32, (SUB, S), 0)
     lane = lax.broadcasted_iota(jnp.int32, (SUB, S), 1)
@@ -312,22 +294,19 @@
         value = jnp.sum(jnp.where(lane == i * SUB + row, total, 0.0), axis=1, keepdims=True)
         v.append(jnp.broadcast_to(value, (SUB, S)))
     a, t = coefficients(v[0], (v[1], v[2]), v[3], (v[4], v[5]), (v[6], v[7]), v[8])
-    sol_stage[...] = (
-        per_lane(a[0]) * zero[...]
-        + per_lane(a[1]) * rot_zero[...]
-        + per_lane(t[0]) * first[...]
-        + per_lane(t[1]) * rot_first[...]
-    )
-    sol_copy = pltpu.make_async_copy(sol_stage, sol, sems.at[0])
-    sol_copy.start()
     keep = (1.0 - mass_shift * a[0], -mass_shift * a[1])
     mixed = plus(scaled(mass_shift, t), a)
-    rows = []
+    sol_rows = []
+    res_rows = []
     for r in range(RHS):
         at = lambda u: (u[0][r : r + 1, :], u[1][r : r + 1, :])
         b, u, w = halves(zero_t, r), halves(first_t, r), halves(second_t, r)
-        rows += list(minus(minus(times(at(keep), b), times(at(mixed), u)), times(at(t), w)))
-    res_stage[...] = jnp.concatenate(rows, axis=0).T
+        sol_rows += list(plus(times(at(a), b), times(at(t), u)))
+        res_rows += list(minus(minus(times(at(keep), b), times(at(mixed), u)), times(at(t), w)))
+    sol_stage[...] = jnp.concatenate(sol_rows, axis=0).T
+    sol_copy = pltpu.make_async_copy(sol_stage, sol, sems.at[0])
+    sol_copy.start()
+    res_stage[...] = jnp.concatenate(res_rows, axis=0).T
     res_copy = pltpu.make_async_copy(res_stage, res, sems.at[1])
     res_copy.start()
     sol_copy.wait()
@@ -385,16 +364,18 @@
         first_body(edge), ((VEC, S), (S, VEC)) + FACES, EDGE_SCRATCH
     )(b, sent[edge], links, part)
     xs, sent = halo(u, faces, ORDERS[1])
-    part, b_rot, u_rot = local_part(n_x, True)(u, *xs, links, b)
+    (part,) = local_part(n_x, True)(u_t, *xs, links)
     for edge in EDGES[1][:-1]:
         part = add_edge(edge, u, sent[edge], links, part)
     edge = EDGES[1][-1]
     w_t, sums = call(
-        lambda *refs: second_body(edge, *refs), ((VEC, S), (devices, 1, S)), EDGE_SCRATCH + (TABLE,)
-    )(u, sent[edge], links, part, u_t, b_t)
+        lambda *refs: second_body(edge, *refs),
+        ((VEC, S), (devices, 1, S)),
+        EDGE_SCRATCH + (TABLE,),
+    )(u, u_t, sent[edge], links, part, b_t)
     sums = lax.all_to_all(sums, AXES, 0, 0)
     sol, res = call(final_body, ((S, VEC),) * 2, FINAL_SCRATCH, None, pl.ANY)(
-        sums, b, b_rot, b_t, u, u_rot, u_t, w_t
+        sums, b_t, u_t, w_t
     )
     return sol.reshape(right_side.shape), res.reshape(right_side.shape)
 

time: 37 us -> 36.1 us (0.976)
  blocking collectives: 11.9 us -> 11.5 us
    all_to_all x1, blocking collectives: 11.9 us -> 11.5 us  [shards(): sums = lax.all_to_all(sums, AXES, 0, 0)]
  transfers between devices with their start and end apart: 10 -> 10, of which waited for: 3 -> 4; matrix products, arithmetic and copies ran while one was open for 0% -> 0% of each run, Pallas kernels for 15% -> 14%
where the time goes in v3:
time: 36.1 us; the launch traced here: 35.9 us
  starting transfers between devices  12.9 us (36%)
  blocking collectives  11.5 us (32%)
  Pallas kernels  7.11 us (20%)
  waiting for transfers between devices  2.56 us (7%)
  local copies, waits for them, and re-layouts  1.14 us (3%)
  between operations  0.79 us (2%)
    ppermute x10, starting transfers between devices, exchange(): lax.ppermute(value, axis, [(i, (i + 1 if (i - offset) % 2 == 0 else i - 1...  12.9 us
    all_to_all x1, blocking collectives, shards(): sums = lax.all_to_all(sums, AXES, 0, 0)  11.5 us
    pallas_call x6, Pallas kernels, add_edge(): return call(body, ((VEC, S),), EDGE_SCRATCH)(*args)[0]  2.61 us
    ppermute x10, waiting for transfers between devices, exchange(): lax.ppermute(value, axis, [(i, (i + 1 if (i - offset) % 2 == 0 else i - 1...  2.56 us
    pallas_call x1, Pallas kernels, shards(): part, b_t = local_part(n_x, False)(b, *xs, links)  1.28 us
    pallas_call x1, Pallas kernels, shards(): part, = local_part(n_x, True)(u_t, *xs, links)  1.18 us
    unnamed x8, local copies, waits for them, and re-layouts  1.14 us
    pallas_call x1, Pallas kernels, shards(): call(final_body, ((S, VEC),) * 2, FINAL_SCRATCH, None, pl.ANY)  0.93 us
  transfers between devices with their start and end apart: 10, of which 4 were waited for; matrix products, arithmetic and copies ran while one was open for 0% of the time, Pallas kernels for 14%

profile of v3, /device:TPU:0, one launch (start us, length us, event | category | flops | bytes accessed | tf_op | source)
XLA Modules:
  0.0 35.9 jit_solution(6859083318490179826)
XLA Ops:
  0.6 0.0 slice-start
  0.6 0.0 slice-start.1
  0.7 0.0 slice-start.2
  0.7 0.6 %collective-permute-start.4 = (f32[128,128]{1,0:T(8,128)}, f32[128,128]{1,0:T(8,128)S(1)}, u32[]{:S(2)}, u32[]{:S(2)}) collective-permute-start(f32[128,128]{1,0:T(8,128)} %bitcast.16), channel_id=1, source_target_pairs={{0,16},{16,0},{1,17},{17,1},{2,18},{18,2},{3,19},{19,3},{4,20},{20... | collective-permute-start | bytes 196616 | tf_op jit(solution)/shard_map/ppermute | solution.py:327
  1.2 0.0 copy-start
  1.2 1.1 %copy-done = f32[1,1,1,128,128]{4,3,2,1,0:T(8,128)S(1)} copy-done((f32[1,1,1,128,128]{4,3,2,1,0:T(8,128)S(1)}, f32[1,1,1,128,128]{4,3,2,1,0:T(8,128)}, u32[]{:S(2)}) %copy-start) | copy-done | bytes 65560
  2.4 3.4 %collective-permute-start.2 = (f32[64,128]{1,0:T(8,128)S(1)}, f32[64,128]{1,0:T(8,128)S(1)}, u32[]{:S(2)}, u32[]{:S(2)}) collective-permute-start(f32[64,128]{1,0:T(8,128)S(1)} %get-tuple-element.20), channel_id=1, source_target_pairs={{0,12},{4,8},{8,4},{12,0},{1,13},{5,9},{9,5},{13,1},{2,14},{6,10},... | collective-permute-start | bytes 98312 | tf_op jit(solution)/shard_map/ppermute | solution.py:327
  5.7 0.5 %collective-permute-start = (f32[64,128]{1,0:T(8,128)S(1)}, f32[64,128]{1,0:T(8,128)S(1)}, u32[]{:S(2)}, u32[]{:S(2)}) collective-permute-start(f32[64,128]{1,0:T(8,128)S(1)} %get-tuple-element.18), channel_id=1, source_target_pairs={{0,4},{4,0},{8,12},{12,8},{1,5},{5,1},{9,13},{13,9},{2,6},{6,2},{1... | collective-permute-start | bytes 98312 | tf_op jit(solution)/shard_map/ppermute | solution.py:327
  6.3 3.6 %collective-permute-start.3 = (f32[16,128]{1,0:T(8,128)S(1)}, f32[16,128]{1,0:T(8,128)S(1)}, u32[]{:S(2)}, u32[]{:S(2)}) collective-permute-start(f32[16,128]{1,0:T(8,128)S(1)} %get-tuple-element.21), channel_id=1, source_target_pairs={{0,3},{1,2},{2,1},{3,0},{4,7},{5,6},{6,5},{7,4},{8,11},{9,10},{10,... | collective-permute-start | bytes 24584 | tf_op jit(solution)/shard_map/ppermute | solution.py:327
  9.9 0.0 collective-permute-start.1
  9.9 0.0 collective-permute-done.4.refs_0_
  9.9 0.0 slice-done
  9.9 0.0 slice-done.1
  9.9 0.0 slice-done.2
  9.9 1.3 %shard_map.42 = (f32[128,128]{1,0:T(8,128)S(1)}, f32[128,128]{1,0:T(8,128)S(1)}) custom-call(f32[128,128]{1,0:T(8,128)S(1)} %bitcast.18, f32[128,128]{1,0:T(8,128)S(1)} %collective-permute-done.4.refs_0_, f32[9,2,32,32,128]{4,3,2,1,0:T(8,128)S(1)} %bitcast.6), custom_call_target="tpu_custom_call" | custom-call | tf_op jit(solution)/shard_map/pallas_call | solution.py:359
  11.2 0.5 %collective-permute-done.3.refs_1_ = f32[16,128]{1,0:T(8,128)S(1)} collective-permute-done((f32[16,128]{1,0:T(8,128)S(1)}, f32[16,128]{1,0:T(8,128)S(1)}, u32[]{:S(2)}, u32[]{:S(2)}) %collective-permute-start.3) | collective-permute-done | bytes 8224 | tf_op jit(solution)/shard_map/ppermute | solution.py:327
  11.7 0.4 %shard_map.43.refs_3_ = f32[128,128]{1,0:T(8,128)S(1)} custom-call(f32[128,128]{1,0:T(8,128)S(1)} %bitcast.19, f32[16,128]{1,0:T(8,128)S(1)} %collective-permute-done.3.refs_1_, f32[9,2,32,32,128]{4,3,2,1,0:T(8,128)S(1)} %bitcast.7, f32[128,128]{1,0:T(8,128)S(1)} %get-tuple-element.22.refs_3_), custom_call_target="tpu_custom_call" | custom-call | tf_op jit(solution)/shard_map/pallas_call | solution.py:151
  12.2 0.0 collective-permute-done.2.refs_1_
  12.2 0.4 %shard_map.44.refs_3_ = f32[128,128]{1,0:T(8,128)S(1)} custom-call(f32[128,128]{1,0:T(8,128)S(1)} %bitcast.20, f32[64,128]{1,0:T(8,128)S(1)} %collective-permute-done.2.refs_1_, f32[9,2,32,32,128]{4,3,2,1,0:T(8,128)S(1)} %bitcast.8, f32[128,128]{1,0:T(8,128)S(1)} %shard_map.43.refs_3_), custom_call_target="tpu_custom_call" | custom-call | tf_op jit(solution)/shard_map/pallas_call | solution.py:151
  12.6 0.9 %collective-permute-done.1.refs_1_ = f32[16,128]{1,0:T(8,128)S(1)} collective-permute-done((f32[16,128]{1,0:T(8,128)S(1)}, f32[16,128]{1,0:T(8,128)S(1)}, u32[]{:S(2)}, u32[]{:S(2)}) %collective-permute-start.1) | collective-permute-done | bytes 8224 | tf_op jit(solution)/shard_map/ppermute | solution.py:327
  13.5 0.4 %shard_map.45.part = f32[128,128]{1,0:T(8,128)S(1)} custom-call(f32[128,128]{1,0:T(8,128)S(1)} %bitcast.21, f32[16,128]{1,0:T(8,128)S(1)} %collective-permute-done.1.refs_1_, f32[9,2,32,32,128]{4,3,2,1,0:T(8,128)S(1)} %bitcast.9, f32[128,128]{1,0:T(8,128)S(1)} %shard_map.44.refs_3_), custom_call_target="tpu_custom_call" | custom-call | tf_op jit(solution)/shard_map/pallas_call | solution.py:151
  14.0 0.0 collective-permute-done.piece
  14.0 0.5 %shard_map.46 = (f32[128,128]{1,0:T(8,128)S(1)}, f32[128,128]{1,0:T(8,128)S(1)}, f32[64,128]{1,0:T(8,128)S(1)}, f32[64,128]{1,0:T(8,128)S(1)}, f32[16,128]{1,0:T(8,128)S(1)}, /*index=5*/f32[16,128]{1,0:T(8,128)S(1)}) custom-call(f32[128,128]{1,0:T(8,128)S(1)} %bitcast.22, f32[64,128]{1,0:T(8,128)S(1)} %collective-permute-done.piece, ...), custom_call_target="tpu_custom_call" | custom-call | tf_op jit(solution)/shard_map/pallas_call | solution.py:363
  14.5 0.1 collective-permute-start.9
  14.6 1.5 %collective-permute-start.8 = (f32[64,128]{1,0:T(8,128)S(1)}, f32[64,128]{1,0:T(8,128)S(1)}, u32[]{:S(2)}, u32[]{:S(2)}) collective-permute-start(f32[64,128]{1,0:T(8,128)S(1)} %get-tuple-element.28), channel_id=1, source_target_pairs={{0,12},{4,8},{8,4},{12,0},{1,13},{5,9},{9,5},{13,1},{2,14},{6,10},... | collective-permute-start | bytes 98312 | tf_op jit(solution)/shard_map/ppermute | solution.py:327
  16.1 0.5 %collective-permute-start.7 = (f32[64,128]{1,0:T(8,128)S(1)}, f32[64,128]{1,0:T(8,128)S(1)}, u32[]{:S(2)}, u32[]{:S(2)}) collective-permute-start(f32[64,128]{1,0:T(8,128)S(1)} %get-tuple-element.27), channel_id=1, source_target_pairs={{0,4},{4,0},{8,12},{12,8},{1,5},{5,1},{9,13},{13,9},{2,6},{6,2},{1... | collective-permute-start | bytes 98312 | tf_op jit(solution)/shard_map/ppermute | solution.py:327
  16.6 2.7 %collective-permute-start.6 = (f32[16,128]{1,0:T(8,128)S(1)}, f32[16,128]{1,0:T(8,128)S(1)}, u32[]{:S(2)}, u32[]{:S(2)}) collective-permute-start(f32[16,128]{1,0:T(8,128)S(1)} %get-tuple-element.26), channel_id=1, source_target_pairs={{0,3},{1,2},{2,1},{3,0},{4,7},{5,6},{6,5},{7,4},{8,11},{9,10},{10,... | collective-permute-start | bytes 24584 | tf_op jit(solution)/shard_map/ppermute | solution.py:327
  19.3 0.0 collective-permute-start.5
  19.3 0.0 collective-permute-done.9.refs_0_
  19.3 1.2 %shard_map.47.refs_3_ = f32[128,128]{1,0:T(8,128)S(1)} custom-call(f32[128,128]{1,0:T(8,128)S(1)} %get-tuple-element.24.src.refs_1_.first_t, f32[128,128]{1,0:T(8,128)S(1)} %collective-permute-done.9.refs_0_, f32[9,2,32,32,128]{4,3,2,1,0:T(8,128)S(1)} %bitcast.11), custom_call_target="tpu_custom_call" | custom-call | tf_op jit(solution)/shard_map/pallas_call | solution.py:367
  20.5 0.0 collective-permute-done.8.refs_1_
  20.5 0.4 %shard_map.48.refs_3_ = f32[128,128]{1,0:T(8,128)S(1)} custom-call(f32[128,128]{1,0:T(8,128)S(1)} %get-tuple-element.23.refs_0_, f32[64,128]{1,0:T(8,128)S(1)} %collective-permute-done.8.refs_1_, f32[9,2,32,32,128]{4,3,2,1,0:T(8,128)S(1)} %bitcast.12, f32[128,128]{1,0:T(8,128)S(1)} %shard_map.47.refs_3_), custom_call_target="tpu_custom_call" | custom-call | tf_op jit(solution)/shard_map/pallas_call | solution.py:151
  21.0 0.0 collective-permute-done.7.refs_1_
  21.0 0.4 %shard_map.49.refs_3_ = f32[128,128]{1,0:T(8,128)S(1)} custom-call(f32[128,128]{1,0:T(8,128)S(1)} %get-tuple-element.23.refs_0_, f32[64,128]{1,0:T(8,128)S(1)} %collective-permute-done.7.refs_1_, f32[9,2,32,32,128]{4,3,2,1,0:T(8,128)S(1)} %bitcast.13, f32[128,128]{1,0:T(8,128)S(1)} %shard_map.48.refs_3_), custom_call_target="tpu_custom_call" | custom-call | tf_op jit(solution)/shard_map/pallas_call | solution.py:151
  21.4 0.7 %collective-permute-done.6.refs_1_ = f32[16,128]{1,0:T(8,128)S(1)} collective-permute-done((f32[16,128]{1,0:T(8,128)S(1)}, f32[16,128]{1,0:T(8,128)S(1)}, u32[]{:S(2)}, u32[]{:S(2)}) %collective-permute-start.6) | collective-permute-done | bytes 8224 | tf_op jit(solution)/shard_map/ppermute | solution.py:327
  22.1 0.4 %shard_map.50.refs_4_ = f32[128,128]{1,0:T(8,128)S(1)} custom-call(f32[128,128]{1,0:T(8,128)S(1)} %get-tuple-element.23.refs_0_, f32[16,128]{1,0:T(8,128)S(1)} %collective-permute-done.6.refs_1_, f32[9,2,32,32,128]{4,3,2,1,0:T(8,128)S(1)} %bitcast.14, f32[128,128]{1,0:T(8,128)S(1)} %shard_map.49.refs_3_), custom_call_target="tpu_custom_call" | custom-call | tf_op jit(solution)/shard_map/pallas_call | solution.py:151
  22.5 0.5 %collective-permute-done.5.refs_2_ = f32[16,128]{1,0:T(8,128)S(1)} collective-permute-done((f32[16,128]{1,0:T(8,128)S(1)}, f32[16,128]{1,0:T(8,128)S(1)}, u32[]{:S(2)}, u32[]{:S(2)}) %collective-permute-start.5) | collective-permute-done | bytes 8224 | tf_op jit(solution)/shard_map/ppermute | solution.py:327
  23.0 0.6 %shard_map.51 = (f32[128,128]{1,0:T(8,128)S(1)}, f32[32,1,128]{2,1,0:T(1,128)S(1)}) custom-call(f32[128,128]{1,0:T(8,128)S(1)} %get-tuple-element.23.refs_0_, f32[128,128]{1,0:T(8,128)S(1)} %get-tuple-element.24.src.refs_1_.first_t, f32[16,128]{1,0:T(8,128)S(1)} %collective-permute-done.5.refs_2_, f32[9,2,32,32,128]{4,3,2,1,0:T(8,128)S(1)} %bitcast.15, ...), custom_call_target="tpu_custom_call" | custom-call | tf_op jit(solution)/shard_map/pallas_call | solution.py:371
  23.5 11.5 %all_to_all.5.sums = f32[32,1,128]{2,1,0:T(1,128)S(1)} all-to-all(f32[32,1,128]{2,1,0:T(1,128)S(1)} %get-tuple-element.30), channel_id=1, replica_groups=mesh['xy'=2,'gz'=4,'ta'=4] {'xy','gz','ta'}, dimensions={0} | all-to-all | bytes 32768 | tf_op jit(solution)/shard_map/all_to_all | solution.py:376
  35.0 0.9 %shard_map.52 = (f32[128,128]{1,0:T(8,128)}, f32[128,128]{1,0:T(8,128)}) custom-call(f32[32,1,128]{2,1,0:T(1,128)S(1)} %all_to_all.5.sums, f32[128,128]{1,0:T(8,128)S(1)} %get-tuple-element.29.refs_5_.zero_t, f32[128,128]{1,0:T(8,128)S(1)} %get-tuple-element.24.src.refs_1_.first_t, f32[128,128]{1,0:T(8,128)S(1)} %get-tuple-element.31.second_t), custom_call_target="tpu_custom_call" | custom-call | tf_op jit(solution)/shard_map/pallas_call | solution.py:377
  (2 shorter events, 0.0 us)
Async XLA Ops:
  0.6 9.3 %slice-start = ((s8[9437184]{0:T(1024)(128)(4,1)}), s8[4194304]{0:T(1024)(128)(4,1)S(1)}, s32[]{:S(2)}) async-start(s8[9437184]{0:T(1024)(128)(4,1)} %bitcast.4), calls=%async_computation.1 | async-start | bytes 8388608
  0.6 9.2 %slice-start.1 = ((s8[9437184]{0:T(1024)(128)(4,1)}), s8[4194304]{0:T(1024)(128)(4,1)S(1)}, s32[]{:S(2)}) async-start(s8[9437184]{0:T(1024)(128)(4,1)} %bitcast.4), calls=%async_computation.2 | async-start | bytes 8388608
  0.7 9.2 %slice-start.2 = ((s8[9437184]{0:T(1024)(128)(4,1)}), s8[1048576]{0:T(1024)(128)(4,1)S(1)}, s32[]{:S(2)}) async-start(s8[9437184]{0:T(1024)(128)(4,1)} %bitcast.4), calls=%async_computation.3 | async-start | bytes 2097152
  0.7 9.2 %collective-permute-start.4 = (f32[128,128]{1,0:T(8,128)}, f32[128,128]{1,0:T(8,128)S(1)}, u32[]{:S(2)}, u32[]{:S(2)}) collective-permute-start(f32[128,128]{1,0:T(8,128)} %bitcast.16), channel_id=1, source_target_pairs={{0,16},{16,0},{1,17},{17,1},{2,18},{18,2},{3,19},{19,3},{4,20},{20... | collective-permute-start | bytes 196616 | tf_op jit(solution)/shard_map/ppermute | solution.py:327
  1.2 1.1 %copy-start = (f32[1,1,1,128,128]{4,3,2,1,0:T(8,128)S(1)}, f32[1,1,1,128,128]{4,3,2,1,0:T(8,128)}, u32[]{:S(2)}) copy-start(f32[1,1,1,128,128]{4,3,2,1,0:T(8,128)} %param.2) | copy-start | bytes 196612
  2.4 9.8 %collective-permute-start.2 = (f32[64,128]{1,0:T(8,128)S(1)}, f32[64,128]{1,0:T(8,128)S(1)}, u32[]{:S(2)}, u32[]{:S(2)}) collective-permute-start(f32[64,128]{1,0:T(8,128)S(1)} %get-tuple-element.20), channel_id=1, source_target_pairs={{0,12},{4,8},{8,4},{12,0},{1,13},{5,9},{9,5},{13,1},{2,14},{6,10},... | collective-permute-start | bytes 98312 | tf_op jit(solution)/shard_map/ppermute | solution.py:327
  5.7 8.2 %collective-permute-start = (f32[64,128]{1,0:T(8,128)S(1)}, f32[64,128]{1,0:T(8,128)S(1)}, u32[]{:S(2)}, u32[]{:S(2)}) collective-permute-start(f32[64,128]{1,0:T(8,128)S(1)} %get-tuple-element.18), channel_id=1, source_target_pairs={{0,4},{4,0},{8,12},{12,8},{1,5},{5,1},{9,13},{13,9},{2,6},{6,2},{1... | collective-permute-start | bytes 98312 | tf_op jit(solution)/shard_map/ppermute | solution.py:327
  6.3 5.4 %collective-permute-start.3 = (f32[16,128]{1,0:T(8,128)S(1)}, f32[16,128]{1,0:T(8,128)S(1)}, u32[]{:S(2)}, u32[]{:S(2)}) collective-permute-start(f32[16,128]{1,0:T(8,128)S(1)} %get-tuple-element.21), channel_id=1, source_target_pairs={{0,3},{1,2},{2,1},{3,0},{4,7},{5,6},{6,5},{7,4},{8,11},{9,10},{10,... | collective-permute-start | bytes 24584 | tf_op jit(solution)/shard_map/ppermute | solution.py:327
  9.9 3.7 %collective-permute-start.1 = (f32[16,128]{1,0:T(8,128)S(1)}, f32[16,128]{1,0:T(8,128)S(1)}, u32[]{:S(2)}, u32[]{:S(2)}) collective-permute-start(f32[16,128]{1,0:T(8,128)S(1)} %get-tuple-element.19), channel_id=1, source_target_pairs={{0,1},{1,0},{2,3},{3,2},{4,5},{5,4},{6,7},{7,6},{8,9},{9,8},{10,11... | collective-permute-start | bytes 24584 | tf_op jit(solution)/shard_map/ppermute | solution.py:327
  14.5 4.8 %collective-permute-start.9 = (f32[128,128]{1,0:T(8,128)S(1)}, f32[128,128]{1,0:T(8,128)S(1)}, u32[]{:S(2)}, u32[]{:S(2)}) collective-permute-start(f32[128,128]{1,0:T(8,128)S(1)} %get-tuple-element.23.refs_0_), channel_id=1, source_target_pairs={{0,16},{16,0},{1,17},{17,1},{2,18},{18,2},{3,19},{19,3},{4,20},{20... | collective-permute-start | bytes 196616 | tf_op jit(solution)/shard_map/ppermute | solution.py:327
  14.6 5.9 %collective-permute-start.8 = (f32[64,128]{1,0:T(8,128)S(1)}, f32[64,128]{1,0:T(8,128)S(1)}, u32[]{:S(2)}, u32[]{:S(2)}) collective-permute-start(f32[64,128]{1,0:T(8,128)S(1)} %get-tuple-element.28), channel_id=1, source_target_pairs={{0,12},{4,8},{8,4},{12,0},{1,13},{5,9},{9,5},{13,1},{2,14},{6,10},... | collective-permute-start | bytes 98312 | tf_op jit(solution)/shard_map/ppermute | solution.py:327
  16.1 4.9 %collective-permute-start.7 = (f32[64,128]{1,0:T(8,128)S(1)}, f32[64,128]{1,0:T(8,128)S(1)}, u32[]{:S(2)}, u32[]{:S(2)}) collective-permute-start(f32[64,128]{1,0:T(8,128)S(1)} %get-tuple-element.27), channel_id=1, source_target_pairs={{0,4},{4,0},{8,12},{12,8},{1,5},{5,1},{9,13},{13,9},{2,6},{6,2},{1... | collective-permute-start | bytes 98312 | tf_op jit(solution)/shard_map/ppermute | solution.py:327
  16.6 5.4 %collective-permute-start.6 = (f32[16,128]{1,0:T(8,128)S(1)}, f32[16,128]{1,0:T(8,128)S(1)}, u32[]{:S(2)}, u32[]{:S(2)}) collective-permute-start(f32[16,128]{1,0:T(8,128)S(1)} %get-tuple-element.26), channel_id=1, source_target_pairs={{0,3},{1,2},{2,1},{3,0},{4,7},{5,6},{6,5},{7,4},{8,11},{9,10},{10,... | collective-permute-start | bytes 24584 | tf_op jit(solution)/shard_map/ppermute | solution.py:327
  19.3 3.7 %collective-permute-start.5 = (f32[16,128]{1,0:T(8,128)S(1)}, f32[16,128]{1,0:T(8,128)S(1)}, u32[]{:S(2)}, u32[]{:S(2)}) collective-permute-start(f32[16,128]{1,0:T(8,128)S(1)} %get-tuple-element.25), channel_id=1, source_target_pairs={{0,1},{1,0},{2,3},{3,2},{4,5},{5,4},{6,7},{7,6},{8,9},{9,8},{10,11... | collective-permute-start | bytes 24584 | tf_op jit(solution)/shard_map/ppermute | solution.py:327

commit v4 on v3

--- a/solution.py
+++ b/solution.py
@@ -22,7 +22,7 @@
 epsilon = 1e-06
 f32 = jnp.float32
 LOCAL_UNROLL = True
-EDGES = (("tb", "zb", "ta", "za"), ("zb", "za", "tb", "ta"))
+EDGES = (("tb", "zb", "ta", "za"), ("tb", "ta"))
 ORDERS = (("tb", "x", "zb", "ta", "za"), ("zb", "x", "za", "tb", "ta"))
 FIRST_COST = 20_000_000_000
 
@@ -143,12 +143,21 @@
     multiply(fields, links, ((0, (first + down,)),), red, out_t, part, True)
 
 
-EDGE_SCRATCH = (pltpu.VMEM((1, VEC, S), f32), RED, PAD)
+EDGE_SCRATCH = (pltpu.VMEM((2, VEC, S), f32), RED, PAD)
 
 
 def add_edge(edge, *args):
     body = lambda *refs: edge_part(edge, *refs)
     return call(body, ((VEC, S),), EDGE_SCRATCH)(*args)[0]
+
+
+def both_z(src, zb, za, links, part, out_t, fields, red, pad):
+    dirs = ()
+    for at, piece in enumerate((zb, za)):
+        down = (lax.axis_index("gz") + 1 - at) % 2
+        fields[at] = assemble_z(src[...], piece[...], down == 0)
+        dirs += ((at, (5 + down,)),)
+    multiply(fields, links, dirs, red, out_t, part, True)
 
 
 def local_part(n_x, second):
@@ -365,6 +374,9 @@
     )(b, sent[edge], links, part)
     xs, sent = halo(u, faces, ORDERS[1])
     (part,) = local_part(n_x, True)(u_t, *xs, links)
+    (part,) = call(both_z, ((VEC, S),), EDGE_SCRATCH)(
+        u, sent["zb"], sent["za"], links, part
+    )
     for edge in EDGES[1][:-1]:
         part = add_edge(edge, u, sent[edge], links, part)
     edge = EDGES[1][-1]

time: 36.1 us -> 36.1 us (level)
    pallas_call x6 -> x4, Pallas kernels: 2.61 us -> 1.74 us  [add_edge(): return call(body, ((VEC, S),), EDGE_SCRATCH)(*args)[0]]
    pallas_call x0 -> x1, Pallas kernels: none -> 0.71 us  [shards(): call(both_z, ((VEC, S),), EDGE_SCRATCH)]
where the time goes in v4:
time: 36.1 us; the launch traced here: 35.9 us
  starting transfers between devices  12.9 us (36%)
  blocking collectives  11.5 us (32%)
  Pallas kernels  6.94 us (19%)
  waiting for transfers between devices  2.73 us (8%)
  local copies, waits for them, and re-layouts  1.14 us (3%)
  between operations  0.78 us (2%)
    ppermute x10, starting transfers between devices, exchange(): lax.ppermute(value, axis, [(i, (i + 1 if (i - offset) % 2 == 0 else i - 1...  12.9 us
    all_to_all x1, blocking collectives, shards(): sums = lax.all_to_all(sums, AXES, 0, 0)  11.5 us
    ppermute x10, waiting for transfers between devices, exchange(): lax.ppermute(value, axis, [(i, (i + 1 if (i - offset) % 2 == 0 else i - 1...  2.73 us
    pallas_call x4, Pallas kernels, add_edge(): return call(body, ((VEC, S),), EDGE_SCRATCH)(*args)[0]  1.74 us
    pallas_call x1, Pallas kernels, shards(): part, b_t = local_part(n_x, False)(b, *xs, links)  1.28 us
    pallas_call x1, Pallas kernels, shards(): part, = local_part(n_x, True)(u_t, *xs, links)  1.18 us
    unnamed x8, local copies, waits for them, and re-layouts  1.14 us
    pallas_call x1, Pallas kernels, shards(): call(final_body, ((S, VEC),) * 2, FINAL_SCRATCH, None, pl.ANY)  0.93 us
  transfers between devices with their start and end apart: 10, of which 4 were waited for; matrix products, arithmetic and copies ran while one was open for 0% of the time, Pallas kernels for 14%

profile of v4, /device:TPU:0, one launch (start us, length us, event | category | flops | bytes accessed | tf_op | source)
XLA Modules:
  0.0 35.9 jit_solution(5419941956647071453)
XLA Ops:
  0.6 0.0 slice-start
  0.6 0.0 slice-start.1
  0.7 0.0 slice-start.2
  0.7 0.6 %collective-permute-start.4 = (f32[128,128]{1,0:T(8,128)}, f32[128,128]{1,0:T(8,128)S(1)}, u32[]{:S(2)}, u32[]{:S(2)}) collective-permute-start(f32[128,128]{1,0:T(8,128)} %bitcast.15), channel_id=1, source_target_pairs={{0,16},{16,0},{1,17},{17,1},{2,18},{18,2},{3,19},{19,3},{4,20},{20... | collective-permute-start | bytes 196616 | tf_op jit(solution)/shard_map/ppermute | solution.py:336
  1.2 0.0 copy-start
  1.2 1.1 %copy-done = f32[1,1,1,128,128]{4,3,2,1,0:T(8,128)S(1)} copy-done((f32[1,1,1,128,128]{4,3,2,1,0:T(8,128)S(1)}, f32[1,1,1,128,128]{4,3,2,1,0:T(8,128)}, u32[]{:S(2)}) %copy-start) | copy-done | bytes 65560
  2.4 3.4 %collective-permute-start.2 = (f32[64,128]{1,0:T(8,128)S(1)}, f32[64,128]{1,0:T(8,128)S(1)}, u32[]{:S(2)}, u32[]{:S(2)}) collective-permute-start(f32[64,128]{1,0:T(8,128)S(1)} %get-tuple-element.20), channel_id=1, source_target_pairs={{0,12},{4,8},{8,4},{12,0},{1,13},{5,9},{9,5},{13,1},{2,14},{6,10},... | collective-permute-start | bytes 98312 | tf_op jit(solution)/shard_map/ppermute | solution.py:336
  5.7 0.5 %collective-permute-start = (f32[64,128]{1,0:T(8,128)S(1)}, f32[64,128]{1,0:T(8,128)S(1)}, u32[]{:S(2)}, u32[]{:S(2)}) collective-permute-start(f32[64,128]{1,0:T(8,128)S(1)} %get-tuple-element.18), channel_id=1, source_target_pairs={{0,4},{4,0},{8,12},{12,8},{1,5},{5,1},{9,13},{13,9},{2,6},{6,2},{1... | collective-permute-start | bytes 98312 | tf_op jit(solution)/shard_map/ppermute | solution.py:336
  6.3 3.6 %collective-permute-start.3 = (f32[16,128]{1,0:T(8,128)S(1)}, f32[16,128]{1,0:T(8,128)S(1)}, u32[]{:S(2)}, u32[]{:S(2)}) collective-permute-start(f32[16,128]{1,0:T(8,128)S(1)} %get-tuple-element.21), channel_id=1, source_target_pairs={{0,3},{1,2},{2,1},{3,0},{4,7},{5,6},{6,5},{7,4},{8,11},{9,10},{10,... | collective-permute-start | bytes 24584 | tf_op jit(solution)/shard_map/ppermute | solution.py:336
  9.9 0.0 collective-permute-start.1
  9.9 0.0 collective-permute-done.4.refs_0_
  9.9 0.0 slice-done
  9.9 0.0 slice-done.1
  9.9 0.0 slice-done.2
  9.9 1.3 %shard_map.42 = (f32[128,128]{1,0:T(8,128)S(1)}, f32[128,128]{1,0:T(8,128)S(1)}) custom-call(f32[128,128]{1,0:T(8,128)S(1)} %bitcast.17, f32[128,128]{1,0:T(8,128)S(1)} %collective-permute-done.4.refs_0_, f32[9,2,32,32,128]{4,3,2,1,0:T(8,128)S(1)} %bitcast.6), custom_call_target="tpu_custom_call" | custom-call | tf_op jit(solution)/shard_map/pallas_call | solution.py:368
  11.2 0.5 %collective-permute-done.3.refs_1_ = f32[16,128]{1,0:T(8,128)S(1)} collective-permute-done((f32[16,128]{1,0:T(8,128)S(1)}, f32[16,128]{1,0:T(8,128)S(1)}, u32[]{:S(2)}, u32[]{:S(2)}) %collective-permute-start.3) | collective-permute-done | bytes 8224 | tf_op jit(solution)/shard_map/ppermute | solution.py:336
  11.7 0.4 %shard_map.43.refs_3_ = f32[128,128]{1,0:T(8,128)S(1)} custom-call(f32[128,128]{1,0:T(8,128)S(1)} %bitcast.18, f32[16,128]{1,0:T(8,128)S(1)} %collective-permute-done.3.refs_1_, f32[9,2,32,32,128]{4,3,2,1,0:T(8,128)S(1)} %bitcast.7, f32[128,128]{1,0:T(8,128)S(1)} %get-tuple-element.22.refs_3_), custom_call_target="tpu_custom_call" | custom-call | tf_op jit(solution)/shard_map/pallas_call | solution.py:151
  12.2 0.0 collective-permute-done.2.refs_1_
  12.2 0.4 %shard_map.44.refs_3_ = f32[128,128]{1,0:T(8,128)S(1)} custom-call(f32[128,128]{1,0:T(8,128)S(1)} %bitcast.19, f32[64,128]{1,0:T(8,128)S(1)} %collective-permute-done.2.refs_1_, f32[9,2,32,32,128]{4,3,2,1,0:T(8,128)S(1)} %bitcast.8, f32[128,128]{1,0:T(8,128)S(1)} %shard_map.43.refs_3_), custom_call_target="tpu_custom_call" | custom-call | tf_op jit(solution)/shard_map/pallas_call | solution.py:151
  12.6 0.9 %collective-permute-done.1.refs_1_ = f32[16,128]{1,0:T(8,128)S(1)} collective-permute-done((f32[16,128]{1,0:T(8,128)S(1)}, f32[16,128]{1,0:T(8,128)S(1)}, u32[]{:S(2)}, u32[]{:S(2)}) %collective-permute-start.1) | collective-permute-done | bytes 8224 | tf_op jit(solution)/shard_map/ppermute | solution.py:336
  13.5 0.4 %shard_map.45.part = f32[128,128]{1,0:T(8,128)S(1)} custom-call(f32[128,128]{1,0:T(8,128)S(1)} %bitcast.20, f32[16,128]{1,0:T(8,128)S(1)} %collective-permute-done.1.refs_1_, f32[9,2,32,32,128]{4,3,2,1,0:T(8,128)S(1)} %bitcast.9, f32[128,128]{1,0:T(8,128)S(1)} %shard_map.44.refs_3_), custom_call_target="tpu_custom_call" | custom-call | tf_op jit(solution)/shard_map/pallas_call | solution.py:151
  14.0 0.0 collective-permute-done.piece
  14.0 0.5 %shard_map.46 = (f32[128,128]{1,0:T(8,128)S(1)}, f32[128,128]{1,0:T(8,128)S(1)}, f32[64,128]{1,0:T(8,128)S(1)}, f32[64,128]{1,0:T(8,128)S(1)}, f32[16,128]{1,0:T(8,128)S(1)}, /*index=5*/f32[16,128]{1,0:T(8,128)S(1)}) custom-call(f32[128,128]{1,0:T(8,128)S(1)} %bitcast.21, f32[64,128]{1,0:T(8,128)S(1)} %collective-permute-done.piece, ...), custom_call_target="tpu_custom_call" | custom-call | tf_op jit(solution)/shard_map/pallas_call | solution.py:372
  14.5 0.1 collective-permute-start.9
  14.6 1.5 %collective-permute-start.7 = (f32[64,128]{1,0:T(8,128)S(1)}, f32[64,128]{1,0:T(8,128)S(1)}, u32[]{:S(2)}, u32[]{:S(2)}) collective-permute-start(f32[64,128]{1,0:T(8,128)S(1)} %get-tuple-element.27), channel_id=1, source_target_pairs={{0,12},{4,8},{8,4},{12,0},{1,13},{5,9},{9,5},{13,1},{2,14},{6,10},... | collective-permute-start | bytes 98312 | tf_op jit(solution)/shard_map/ppermute | solution.py:336
  16.1 0.5 %collective-permute-start.8 = (f32[64,128]{1,0:T(8,128)S(1)}, f32[64,128]{1,0:T(8,128)S(1)}, u32[]{:S(2)}, u32[]{:S(2)}) collective-permute-start(f32[64,128]{1,0:T(8,128)S(1)} %get-tuple-element.28), channel_id=1, source_target_pairs={{0,4},{4,0},{8,12},{12,8},{1,5},{5,1},{9,13},{13,9},{2,6},{6,2},{1... | collective-permute-start | bytes 98312 | tf_op jit(solution)/shard_map/ppermute | solution.py:336
  16.6 2.7 %collective-permute-start.6 = (f32[16,128]{1,0:T(8,128)S(1)}, f32[16,128]{1,0:T(8,128)S(1)}, u32[]{:S(2)}, u32[]{:S(2)}) collective-permute-start(f32[16,128]{1,0:T(8,128)S(1)} %get-tuple-element.26), channel_id=1, source_target_pairs={{0,3},{1,2},{2,1},{3,0},{4,7},{5,6},{6,5},{7,4},{8,11},{9,10},{10,... | collective-permute-start | bytes 24584 | tf_op jit(solution)/shard_map/ppermute | solution.py:336
  19.3 0.0 collective-permute-start.5
  19.3 0.0 collective-permute-done.9.refs_0_
  19.3 1.2 %shard_map.47.part = f32[128,128]{1,0:T(8,128)S(1)} custom-call(f32[128,128]{1,0:T(8,128)S(1)} %get-tuple-element.24.src.refs_1_.first_t, f32[128,128]{1,0:T(8,128)S(1)} %collective-permute-done.9.refs_0_, f32[9,2,32,32,128]{4,3,2,1,0:T(8,128)S(1)} %bitcast.11), custom_call_target="tpu_custom_call" | custom-call | tf_op jit(solution)/shard_map/pallas_call | solution.py:376
  20.5 0.0 collective-permute-done.7.zb
  20.5 0.0 collective-permute-done.8.za
  20.5 0.7 %shard_map.48.refs_3_ = f32[128,128]{1,0:T(8,128)S(1)} custom-call(f32[128,128]{1,0:T(8,128)S(1)} %get-tuple-element.23.src.refs_0_, f32[64,128]{1,0:T(8,128)S(1)} %collective-permute-done.7.zb, f32[64,128]{1,0:T(8,128)S(1)} %collective-permute-done.8.za, f32[9,2,32,32,128]{4,3,2,1,0:T(8,128)S(1)} %bitcast.12, f32[128,128]{1,0:T(8,128)S(1)} %shard_map.47.part), custom_call_target="tpu_custom_call" | custom-call | tf_op jit(solution)/shard_map/pallas_call | solution.py:377
  21.2 0.8 %collective-permute-done.6.refs_1_ = f32[16,128]{1,0:T(8,128)S(1)} collective-permute-done((f32[16,128]{1,0:T(8,128)S(1)}, f32[16,128]{1,0:T(8,128)S(1)}, u32[]{:S(2)}, u32[]{:S(2)}) %collective-permute-start.6) | collective-permute-done | bytes 8224 | tf_op jit(solution)/shard_map/ppermute | solution.py:336
  22.1 0.4 %shard_map.49.refs_4_ = f32[128,128]{1,0:T(8,128)S(1)} custom-call(f32[128,128]{1,0:T(8,128)S(1)} %get-tuple-element.23.src.refs_0_, f32[16,128]{1,0:T(8,128)S(1)} %collective-permute-done.6.refs_1_, f32[9,2,32,32,128]{4,3,2,1,0:T(8,128)S(1)} %bitcast.13, f32[128,128]{1,0:T(8,128)S(1)} %shard_map.48.refs_3_), custom_call_target="tpu_custom_call" | custom-call | tf_op jit(solution)/shard_map/pallas_call | solution.py:151
  22.5 0.5 %collective-permute-done.5.refs_2_ = f32[16,128]{1,0:T(8,128)S(1)} collective-permute-done((f32[16,128]{1,0:T(8,128)S(1)}, f32[16,128]{1,0:T(8,128)S(1)}, u32[]{:S(2)}, u32[]{:S(2)}) %collective-permute-start.5) | collective-permute-done | bytes 8224 | tf_op jit(solution)/shard_map/ppermute | solution.py:336
  23.0 0.6 %shard_map.50 = (f32[128,128]{1,0:T(8,128)S(1)}, f32[32,1,128]{2,1,0:T(1,128)S(1)}) custom-call(f32[128,128]{1,0:T(8,128)S(1)} %get-tuple-element.23.src.refs_0_, f32[128,128]{1,0:T(8,128)S(1)} %get-tuple-element.24.src.refs_1_.first_t, f32[16,128]{1,0:T(8,128)S(1)} %collective-permute-done.5.refs_2_, f32[9,2,32,32,128]{4,3,2,1,0:T(8,128)S(1)} %bitcast.14, ...), custom_call_target="tpu_custom_call" | custom-call | tf_op jit(solution)/shard_map/pallas_call | solution.py:383
  23.5 11.5 %all_to_all.5.sums = f32[32,1,128]{2,1,0:T(1,128)S(1)} all-to-all(f32[32,1,128]{2,1,0:T(1,128)S(1)} %get-tuple-element.30), channel_id=1, replica_groups=mesh['xy'=2,'gz'=4,'ta'=4] {'xy','gz','ta'}, dimensions={0} | all-to-all | bytes 32768 | tf_op jit(solution)/shard_map/all_to_all | solution.py:388
  35.0 0.9 %shard_map.51 = (f32[128,128]{1,0:T(8,128)}, f32[128,128]{1,0:T(8,128)}) custom-call(f32[32,1,128]{2,1,0:T(1,128)S(1)} %all_to_all.5.sums, f32[128,128]{1,0:T(8,128)S(1)} %get-tuple-element.29.refs_5_.zero_t, f32[128,128]{1,0:T(8,128)S(1)} %get-tuple-element.24.src.refs_1_.first_t, f32[128,128]{1,0:T(8,128)S(1)} %get-tuple-element.31.second_t), custom_call_target="tpu_custom_call" | custom-call | tf_op jit(solution)/shard_map/pallas_call | solution.py:389
  (2 shorter events, 0.0 us)
Async XLA Ops:
  0.6 9.3 %slice-start = ((s8[9437184]{0:T(1024)(128)(4,1)}), s8[4194304]{0:T(1024)(128)(4,1)S(1)}, s32[]{:S(2)}) async-start(s8[9437184]{0:T(1024)(128)(4,1)} %bitcast.4), calls=%async_computation.1 | async-start | bytes 8388608
  0.6 9.2 %slice-start.1 = ((s8[9437184]{0:T(1024)(128)(4,1)}), s8[4194304]{0:T(1024)(128)(4,1)S(1)}, s32[]{:S(2)}) async-start(s8[9437184]{0:T(1024)(128)(4,1)} %bitcast.4), calls=%async_computation.2 | async-start | bytes 8388608
  0.7 9.2 %slice-start.2 = ((s8[9437184]{0:T(1024)(128)(4,1)}), s8[1048576]{0:T(1024)(128)(4,1)S(1)}, s32[]{:S(2)}) async-start(s8[9437184]{0:T(1024)(128)(4,1)} %bitcast.4), calls=%async_computation.3 | async-start | bytes 2097152
  0.7 9.2 %collective-permute-start.4 = (f32[128,128]{1,0:T(8,128)}, f32[128,128]{1,0:T(8,128)S(1)}, u32[]{:S(2)}, u32[]{:S(2)}) collective-permute-start(f32[128,128]{1,0:T(8,128)} %bitcast.15), channel_id=1, source_target_pairs={{0,16},{16,0},{1,17},{17,1},{2,18},{18,2},{3,19},{19,3},{4,20},{20... | collective-permute-start | bytes 196616 | tf_op jit(solution)/shard_map/ppermute | solution.py:336
  1.2 1.1 %copy-start = (f32[1,1,1,128,128]{4,3,2,1,0:T(8,128)S(1)}, f32[1,1,1,128,128]{4,3,2,1,0:T(8,128)}, u32[]{:S(2)}) copy-start(f32[1,1,1,128,128]{4,3,2,1,0:T(8,128)} %param.2) | copy-start | bytes 196612
  2.4 9.8 %collective-permute-start.2 = (f32[64,128]{1,0:T(8,128)S(1)}, f32[64,128]{1,0:T(8,128)S(1)}, u32[]{:S(2)}, u32[]{:S(2)}) collective-permute-start(f32[64,128]{1,0:T(8,128)S(1)} %get-tuple-element.20), channel_id=1, source_target_pairs={{0,12},{4,8},{8,4},{12,0},{1,13},{5,9},{9,5},{13,1},{2,14},{6,10},... | collective-permute-start | bytes 98312 | tf_op jit(solution)/shard_map/ppermute | solution.py:336
  5.7 8.2 %collective-permute-start = (f32[64,128]{1,0:T(8,128)S(1)}, f32[64,128]{1,0:T(8,128)S(1)}, u32[]{:S(2)}, u32[]{:S(2)}) collective-permute-start(f32[64,128]{1,0:T(8,128)S(1)} %get-tuple-element.18), channel_id=1, source_target_pairs={{0,4},{4,0},{8,12},{12,8},{1,5},{5,1},{9,13},{13,9},{2,6},{6,2},{1... | collective-permute-start | bytes 98312 | tf_op jit(solution)/shard_map/ppermute | solution.py:336
  6.3 5.4 %collective-permute-start.3 = (f32[16,128]{1,0:T(8,128)S(1)}, f32[16,128]{1,0:T(8,128)S(1)}, u32[]{:S(2)}, u32[]{:S(2)}) collective-permute-start(f32[16,128]{1,0:T(8,128)S(1)} %get-tuple-element.21), channel_id=1, source_target_pairs={{0,3},{1,2},{2,1},{3,0},{4,7},{5,6},{6,5},{7,4},{8,11},{9,10},{10,... | collective-permute-start | bytes 24584 | tf_op jit(solution)/shard_map/ppermute | solution.py:336
  9.9 3.7 %collective-permute-start.1 = (f32[16,128]{1,0:T(8,128)S(1)}, f32[16,128]{1,0:T(8,128)S(1)}, u32[]{:S(2)}, u32[]{:S(2)}) collective-permute-start(f32[16,128]{1,0:T(8,128)S(1)} %get-tuple-element.19), channel_id=1, source_target_pairs={{0,1},{1,0},{2,3},{3,2},{4,5},{5,4},{6,7},{7,6},{8,9},{9,8},{10,11... | collective-permute-start | bytes 24584 | tf_op jit(solution)/shard_map/ppermute | solution.py:336
  14.5 4.8 %collective-permute-start.9 = (f32[128,128]{1,0:T(8,128)S(1)}, f32[128,128]{1,0:T(8,128)S(1)}, u32[]{:S(2)}, u32[]{:S(2)}) collective-permute-start(f32[128,128]{1,0:T(8,128)S(1)} %get-tuple-element.23.src.refs_0_), channel_id=1, source_target_pairs={{0,16},{16,0},{1,17},{17,1},{2,18},{18,2},{3,19},{19,3},{4,20},{20... | collective-permute-start | bytes 196616 | tf_op jit(solution)/shard_map/ppermute | solution.py:336
  14.6 5.9 %collective-permute-start.7 = (f32[64,128]{1,0:T(8,128)S(1)}, f32[64,128]{1,0:T(8,128)S(1)}, u32[]{:S(2)}, u32[]{:S(2)}) collective-permute-start(f32[64,128]{1,0:T(8,128)S(1)} %get-tuple-element.27), channel_id=1, source_target_pairs={{0,12},{4,8},{8,4},{12,0},{1,13},{5,9},{9,5},{13,1},{2,14},{6,10},... | collective-permute-start | bytes 98312 | tf_op jit(solution)/shard_map/ppermute | solution.py:336
  16.1 4.4 %collective-permute-start.8 = (f32[64,128]{1,0:T(8,128)S(1)}, f32[64,128]{1,0:T(8,128)S(1)}, u32[]{:S(2)}, u32[]{:S(2)}) collective-permute-start(f32[64,128]{1,0:T(8,128)S(1)} %get-tuple-element.28), channel_id=1, source_target_pairs={{0,4},{4,0},{8,12},{12,8},{1,5},{5,1},{9,13},{13,9},{2,6},{6,2},{1... | collective-permute-start | bytes 98312 | tf_op jit(solution)/shard_map/ppermute | solution.py:336
  16.6 5.4 %collective-permute-start.6 = (f32[16,128]{1,0:T(8,128)S(1)}, f32[16,128]{1,0:T(8,128)S(1)}, u32[]{:S(2)}, u32[]{:S(2)}) collective-permute-start(f32[16,128]{1,0:T(8,128)S(1)} %get-tuple-element.26), channel_id=1, source_target_pairs={{0,3},{1,2},{2,1},{3,0},{4,7},{5,6},{6,5},{7,4},{8,11},{9,10},{10,... | collective-permute-start | bytes 24584 | tf_op jit(solution)/shard_map/ppermute | solution.py:336
  19.3 3.7 %collective-permute-start.5 = (f32[16,128]{1,0:T(8,128)S(1)}, f32[16,128]{1,0:T(8,128)S(1)}, u32[]{:S(2)}, u32[]{:S(2)}) collective-permute-start(f32[16,128]{1,0:T(8,128)S(1)} %get-tuple-element.25), channel_id=1, source_target_pairs={{0,1},{1,0},{2,3},{3,2},{4,5},{5,4},{6,7},{7,6},{8,9},{9,8},{10,11... | collective-permute-start | bytes 24584 | tf_op jit(solution)/shard_map/ppermute | solution.py:336
